TPU v7x, 16 devices: a 4x2x1 block of a 4x4x8 slice. The times are simulated.
16 devices in a mesh: batch: 2 (over y, z), seq: 8 (over x, core).
Axes of the slice: x: 4, y: 2, z: 1, core: 2. Of those that a mesh axis runs over, the one named last changes fastest.
The devices are a block of a 4x4x8 slice.
Arguments:
- hidden: bfloat16 [32, 4, 7168], P('batch'), parts along dimension 0
- cache_lens: int32 [32], P('batch'), parts along dimension 0
- c_kv: bfloat16 [32, 16384, 512], P('batch', 'seq'), parts along dimension 0
- k_r: bfloat16 [32, 16384, 64], P('batch', 'seq'), parts along dimension 0
- w_uq: bfloat16 [7168, 128, 128], P(None, 'seq')
- w_qr: bfloat16 [7168, 128, 64], P(None, 'seq')
- w_uk: bfloat16 [128, 128, 512], P('seq')
- w_uv: bfloat16 [128, 512, 128], P('seq')
- w_o: bfloat16 [128, 128, 7168], P('seq')
Outputs:
- output: bfloat16 [32, 4, 7168], P('batch'), parts along dimension 0
There are 2 independent parts. A program takes and returns all parts, laid end to end along the dimension named above; an argument that names none is the same for every part.
All inputs are finite; a program needn't handle non-finite values.
Results may differ from a plain program's by a relative error of at most 0.00666237.
Values are sent between devices in bfloat16 or wider.
A program may use at most 768 MiB of HBM per device.

v0:
```python
import jax
import jax.numpy as jnp
from jax import lax
from jax.sharding import PartitionSpec as P

MASK_FILL = -1e30


def solution(mesh):
    def local_step(hidden, cache_lens, c_kv, k_r, w_uq, w_qr, w_uk, w_uv, w_o):
        score_scale = (w_uq.shape[2] + w_qr.shape[2]) ** -0.5
        q_nope = jnp.einsum("cre,eil->cril", hidden, w_uq, preferred_element_type=jnp.float32).astype(jnp.bfloat16)
        q_rope = jnp.einsum("cre,eis->cris", hidden, w_qr, preferred_element_type=jnp.float32).astype(jnp.bfloat16)
        q_lat = jnp.einsum("bqhk,hkc->bqhc", q_nope, w_uk, preferred_element_type=jnp.float32).astype(jnp.bfloat16)
        lat_all = lax.all_gather(q_lat, "seq", axis=2, tiled=True)
        rope_all = lax.all_gather(q_rope, "seq", axis=2, tiled=True)
        local_len = c_kv.shape[1]
        positions = lax.axis_index("seq") * local_len + jnp.arange(local_len)
        limits = cache_lens[:, None] + jnp.arange(hidden.shape[1])[None, :]
        visible = positions[None, None, None, :] <= limits[:, :, None, None]
        scores = (jnp.einsum("bqhc,btc->bqht", lat_all, c_kv, preferred_element_type=jnp.float32)
                  + jnp.einsum("bqhr,btr->bqht", rope_all, k_r, preferred_element_type=jnp.float32)) * score_scale
        scores = jnp.where(visible, scores, MASK_FILL)
        local_max = jnp.max(scores, axis=-1)
        weights = jnp.exp(scores - local_max[..., None])
        local_sum = jnp.sum(weights, axis=-1)
        o_part = jnp.einsum("bqht,btc->bqhc", weights.astype(jnp.bfloat16), c_kv, preferred_element_type=jnp.float32)
        global_max = lax.pmax(local_max, "seq")
        rescale = jnp.exp(local_max - global_max)
        o_sum = lax.psum_scatter(o_part * rescale[..., None], "seq", scatter_dimension=2, tiled=True)
        l_sum = lax.psum_scatter(local_sum * rescale, "seq", scatter_dimension=2, tiled=True)
        o_lat = (o_sum / l_sum[..., None]).astype(jnp.bfloat16)
        o_val = jnp.einsum("bqhc,hcv->bqhv", o_lat, w_uv, preferred_element_type=jnp.float32).astype(jnp.bfloat16)
        y_part = jnp.einsum("criw,iwe->cre", o_val, w_o, preferred_element_type=jnp.float32)
        y_sum = lax.psum(y_part, "seq")
        return (hidden.astype(jnp.float32) + y_sum).astype(jnp.bfloat16)

    specs_in = (P("batch", None, None), P("batch"), P("batch", "seq", None), P("batch", "seq", None),
                P(None, "seq", None), P(None, "seq", None), P("seq", None, None), P("seq", None, None),
                P("seq", None, None))
    return jax.shard_map(local_step, mesh=mesh, in_specs=specs_in, out_specs=P("batch", None, None), check_vma=False)
```

profile of v0, /device:TPU:113, one launch (start us, length us, event | category | flops | bytes accessed | tf_op | source)
XLA Modules:
  0.0 407.4 jit_solution(13158271024799046753)
XLA Ops:
  6.6 12.7 %fusion.14 = bf16[16,4,16,64]{3,0,2,1:T(8,128)(2,1)S(1)} fusion(bf16[7168,16,64]{0,2,1:T(8,128)(2,1)} %param.14, bf16[16,4,7168,1]{2,1,0,3:T(4,128)(2,1)} %bitcast.64), kind=kOutput, calls=%fused_computation.13 | convolution fusion | flops 939524096 | bytes 15728640 | tf_op jit(solution)/shard_map/cre,eis->cris/dot_general | solution.py:13
  19.2 0.8 copy.45
  20.1 0.2 all-gather.3.cloned.1.call-start
  20.3 18.2 %fusion.12 = bf16[16,4,16,128]{3,0,2,1:T(8,128)(2,1)S(1)} fusion(bf16[7168,16,128,1]{2,1,0,3:T(8,128)(2,1)} %bitcast.72, bf16[16,4,7168,1]{2,1,0,3:T(4,128)(2,1)S(1)} %bitcast.65), kind=kOutput, calls=%fused_computation.11 | convolution fusion | flops 1879048192 | bytes 30539776 | tf_op jit(solution)/shard_map/cre,eil->cril/dot_general | solution.py:12
  38.7 0.5 fusion.26
  39.2 1.6 copy.47
  40.8 0.3 reduce-scatter.7.cloned.1.call-start
  41.4 4.4 %all-gather.5.cloned.1.call-done = bf16[16,4,128,64]{3,2,1,0:T(8,128)(2,1)} async-done(((bf16[16,4,16,64]{3,2,1,0:T(8,128)(2,1)}), bf16[16,4,128,64]{3,2,1,0:T(8,128)(2,1)}) %all-gather.5.cloned.1.call-update) | async-done | bytes 1048592 | tf_op jit(solution)/shard_map/all_gather | solution.py:16
  45.8 25.6 %fusion.24 = f32[16,4,128,2048]{3,2,1,0:T(8,128)} fusion(bf16[16,4,128,64]{3,2,1,0:T(8,128)(2,1)} %all-gather.5.cloned.1.call-done, bf16[16,2048,64]{1,2,0:T(8,128)(2,1)} %param.12), kind=kOutput, calls=%fused_computation.17 | convolution fusion | flops 2147483648 | bytes 72351744 | tf_op jit(solution)/shard_map/bqhr,btr->bqht/dot_general | solution.py:22
  71.5 22.3 %all-gather.3.cloned.1.call-done = bf16[16,4,128,512]{3,2,1,0:T(8,128)(2,1)} async-done(((bf16[16,4,16,512]{3,2,1,0:T(8,128)(2,1)}), bf16[16,4,128,512]{3,2,1,0:T(8,128)(2,1)}) %all-gather.3.cloned.1.call-update) | async-done | bytes 8388624 | tf_op jit(solution)/shard_map/all_gather | solution.py:15
  93.8 57.1 %fusion.46 = (f32[16,4,128]{2,1,0:T(4,128)S(1)}, f32[16,4,128,2048]{3,2,1,0:T(8,128)}) fusion(f32[16,4,128,2048]{3,2,1,0:T(8,128)} %fusion.24, bf16[16,4,128,512]{3,2,1,0:T(8,128)(2,1)} %all-gather.3.cloned.1.call-done, bf16[16,2048,512]{2,1,0:T(8,128)(2,1)} %param.11, pred[16,4,2048]{2,1,0:T(4,128)(4,1)S(1)} %broadcast_compare_fusion), kind=kOutput, calls=%fused_computation.40 | convolution fusion | flops 17246969856 | bytes 176324608 | tf_op jit(solution)/shard_map/bqhc,btc->bqht/dot_general | solution.py:21
  150.9 20.9 %pmax.7 = f32[16,4,128]{2,1,0:T(4,128)S(1)} all-reduce(f32[16,4,128]{2,1,0:T(4,128)S(1)} %get-tuple-element.7), channel_id=1, replica_groups=mesh['batch'=2,'seq'=8] {'seq'}, use_global_device_ids=true, to_apply=%region_1.2 | all-reduce | flops 8192 | bytes 65536 | tf_op jit(solution)/shard_map/pmax | solution.py:28
  171.8 21.1 %fusion = f32[16,4,128]{2,1,0:T(4,128)S(1)} fusion(f32[16,4,128,2048]{3,2,1,0:T(8,128)} %get-tuple-element.8, f32[16,4,128]{2,1,0:T(4,128)S(1)} %get-tuple-element.7), kind=kLoop, calls=%fused_computation.2 | loop fusion | flops 33546240 | bytes 67174400 | tf_op jit(solution)/shard_map/reduce_sum | solution.py:26
  192.9 0.5 copy.25
  193.5 1.1 reshape.43
  194.7 41.4 %fusion.16 = f32[16,4,128,512]{3,2,1,0:T(8,128)} fusion(bf16[16,2048,512]{2,1,0:T(8,128)(2,1)} %param.11, f32[16,4,128,2048]{3,2,1,0:T(8,128)} %get-tuple-element.8, f32[16,4,128]{2,1,0:T(4,128)S(1)} %get-tuple-element.7, f32[16,4,128]{2,1,0:T(4,128)S(1)} %bitcast.71), kind=kOutput, calls=%fused_computation.15 | convolution fusion | flops 17217617920 | bytes 117506048 | tf_op jit(solution)/shard_map/bqht,btc->bqhc/dot_general | solution.py:27
  236.1 0.3 all-reduce.2.cloned.1.call-start
  236.5 0.8 reshape.44
  237.5 88.0 %reduce-scatter.5.cloned.1.call-done = f32[16,4,16,512]{3,2,1,0:T(8,128)} async-done(((f32[16,4,128,512]{3,2,1,0:T(8,128)}), f32[16,4,16,512]{3,2,1,0:T(8,128)}) %reduce-scatter.5.cloned.1.call-update) | async-done | bytes 2097168 | tf_op jit(solution)/shard_map/reduce_scatter | solution.py:30
  325.4 1.9 divide_convert_fusion
  327.4 14.7 %fusion.21 = f32[16,4,7168]{2,0,1:T(8,128)} fusion(bf16[16,128,7168]{2,1,0:T(8,128)(2,1)} %param.17, bf16[16,512,128]{2,1,0:T(8,128)(2,1)} %param.16, bf16[16,4,16,512]{3,2,1,0:T(8,128)(2,1)S(1)} %divide_convert_fusion), kind=kOutput, calls=%fused_computation.16 | convolution fusion | flops 2013396992 | bytes 34340864 | tf_op jit(solution)/shard_map/criw,iwe->cre/dot_general | solution.py:34
  342.2 54.9 %all-reduce.2.cloned.1.call-done = f32[16,4,7168]{2,0,1:T(8,128)} async-done(((f32[16,4,7168]{2,0,1:T(8,128)}), f32[16,4,7168]{2,0,1:T(8,128)}) %all-reduce.2.cloned.1.call-update) | async-done | bytes 1835024 | tf_op jit(solution)/shard_map/psum | solution.py:35
  397.1 2.1 add_convert_fusion
  399.2 1.6 copy.13
  (22 shorter events, 0.9 us)
Async XLA Ops:
  6.5 32.1 %copy-start = (bf16[16,128,512]{2,1,0:T(8,128)(2,1)S(1)}, bf16[16,128,512]{2,1,0:T(8,128)(2,1)}, u32[]{:S(2)}) copy-start(bf16[16,128,512]{2,1,0:T(8,128)(2,1)} %param.15) | copy-start | bytes 6291460
  6.6 13.8 %copy-start.2 = (bf16[16,4,7168]{2,1,0:T(4,128)(2,1)S(1)}, bf16[16,4,7168]{2,1,0:T(4,128)(2,1)}, u32[]{:S(2)}) copy-start(bf16[16,4,7168]{2,1,0:T(4,128)(2,1)} %param.9) | copy-start | bytes 2752516
  6.6 39.3 %all-gather.5.cloned.1.call-start = ((), (), s32[]{:S(2)}) async-start(), calls=%async_computation.3 | async-start | bytes 2359296 | tf_op jit(solution)/shard_map/all_gather | solution.py:16
  20.1 73.7 %all-gather.3.cloned.1.call-start = ((), (), s32[]{:S(2)}) async-start(), calls=%async_computation.2 | async-start | bytes 9437184 | tf_op jit(solution)/shard_map/all_gather | solution.py:15
  20.3 20.8 %copy-start.3 = (s32[16]{0:T(128)S(1)}, s32[16]{0:T(128)}, u32[]{:S(2)}) copy-start(s32[16]{0:T(128)} %param.10) | copy-start | bytes 196
  40.8 195.6 %reduce-scatter.7.cloned.1.call-start = ((), (), s32[]{:S(2)}) async-start(), calls=%async_computation.6 | async-start | bytes 73728
  194.6 130.8 %reduce-scatter.5.cloned.1.call-start = ((), (), s32[]{:S(2)}) async-start(), calls=%async_computation.4 | async-start | bytes 18874368 | tf_op jit(solution)/shard_map/reduce_scatter | solution.py:30
  236.1 161.0 %all-reduce.2.cloned.1.call-start = ((), (), s32[]{:S(2)}) async-start(), calls=%async_computation.5 | async-start | bytes 3670016 | tf_op jit(solution)/shard_map/psum | solution.py:35
  325.4 75.4 %copy-start.1 = (bf16[16,128,512]{2,1,0:T(8,128)(2,1)S(1)}, bf16[16,128,512]{2,1,0:T(8,128)(2,1)}, u32[]{:S(2)}) copy-start(bf16[16,128,512]{2,1,0:T(8,128)(2,1)} %param.15) | copy-start | bytes 6291460
Sparse Core Ops, SparseCore 0:
  20.2 25.6 all-gather.4
  47.4 46.3 all-gather.2
  194.7 25.6 reduce-scatter.6
  236.2 89.1 reduce-scatter.4
  342.3 54.7 all-reduce.1
where the time goes:
time: 410 us; the launch traced here: 407 us
  matrix products  170 us (41%)
  waiting for transfers between devices  170 us (41%)
  other arithmetic  25.4 us (6%)
  blocking collectives  20.9 us (5%)
  between operations  13.3 us (3%)
  local copies, waits for them, and re-layouts  6.65 us (2%)
    reduce_scatter x1, waiting for transfers between devices, local_step(): lax.psum_scatter(o_part * rescale[..., None], 'seq', scatter_dimension=2,...  88 us
    dot_general x1, matrix products, local_step(): jnp.einsum('bqhc,btc->bqht', lat_all, c_kv, preferred_element_type=jnp.fl...  57.1 us
    psum x1, waiting for transfers between devices, local_step(): y_sum = lax.psum(y_part, 'seq')  54.9 us
    dot_general x1, matrix products, local_step(): jnp.einsum('bqht,btc->bqhc', weights.astype(jnp.bfloat16), c_kv, preferre...  41.4 us
    dot_general x1, matrix products, local_step(): jnp.einsum('bqhr,btr->bqht', rope_all, k_r, preferred_element_type=jnp.fl...  25.6 us
    all_gather x1, waiting for transfers between devices, local_step(): lat_all = lax.all_gather(q_lat, 'seq', axis=2, tiled=True)  22.3 us
    reduce_sum x1, other arithmetic, local_step(): local_sum = jnp.sum(weights, axis=-1)  21.1 us
    pmax x1, blocking collectives, local_step(): global_max = lax.pmax(local_max, 'seq')  20.9 us
  transfers between devices with their start and end apart: 5, of which 4 were waited for; matrix products, arithmetic and copies ran while one was open for 22% of the time, Pallas kernels for 0%

commit v1 on v0

v1 whole, which is shorter than its diff:
```python
import functools

import jax
import jax.numpy as jnp
from jax import lax
from jax.experimental import pallas as pl
from jax.experimental.pallas import tpu as pltpu
from jax.sharding import PartitionSpec as P

MASK_FILL = -1e30
LOG2E = 1.4426950408889634
MESH = pl.DeviceIdType.MESH
LAG_B, LAG_C, LAG_D = 1, 3, 5
PIECES = 4


def remote(src, dst, send_sem, recv_sem, dev):
    return pltpu.make_async_remote_copy(src_ref=src, dst_ref=dst, send_sem=send_sem, recv_sem=recv_sem,
                                        device_id={"seq": dev}, device_id_type=MESH)


def place(chips):
    me = lax.axis_index("seq")
    x, c = me // 2, lax.rem(me, 2)
    xr, xl = lax.rem(x + 1, chips), lax.rem(x + chips - 1, chips)
    return x, c, xr, xl, 2 * xr + c, 2 * xl + c, 2 * x + 1 - c


def greet(devs):
    barrier = pltpu.get_barrier_semaphore()
    for dev in devs:
        pl.semaphore_signal(barrier, inc=1, device_id={"seq": dev}, device_id_type=MESH)
    pl.semaphore_wait(barrier, len(devs))


def gather_kernel(chips, lat_ref, rope_ref, lat_all, rope_all, send, recv, local):
    x, c, xr, xl, right, left, partner = place(chips)
    xo = lax.rem(x + 2, chips)
    step = lat_ref.shape[0] // PIECES
    pairs = ((lat_ref, lat_all), (rope_ref, rope_all))
    half = PIECES // 2
    greet((right, left, partner))
    rows = lambda p: pl.ds(p * step, step)

    def copy(a, p, kind, src, slot, dev):
        return remote(src, pairs[a][1].at[rows(p), slot[1], slot[0]], send.at[a, p, kind], recv.at[a, p, kind], dev)

    def own(a, p, kind, dev):
        return copy(a, p, kind, pairs[a][0].at[rows(p)], (x, c), dev)

    def pass_on(a, p, kind, block, dev):
        return copy(a, p, kind, pairs[a][1].at[rows(p), c, block], (block, c), dev)

    def landed(a, p, kind, block, core):
        ref = pairs[a][1].at[rows(p), core, block]
        return remote(ref, ref, send.at[a, p, kind], recv.at[a, p, kind], partner)

    keep = lambda a: pltpu.make_async_copy(pairs[a][0], pairs[a][1].at[:, c, x], local.at[a])
    order_l = [(p + half) % PIECES for p in range(PIECES)]
    for i in range(PIECES):
        for a in range(2):
            own(a, i, 0, right).start()
            own(a, order_l[i], 1, left).start()
    for p in range(PIECES):
        for a in range(2):
            own(a, p, 2, partner).start()
    for a in range(2):
        keep(a).start()
    for i in range(PIECES):
        for a in range(2):
            landed(a, i, 0, xl, c).wait_recv()
            if i < half:
                pass_on(a, i, 3, xl, right).start()
            pass_on(a, i, 4, xl, partner).start()
            p = order_l[i]
            landed(a, p, 1, xr, c).wait_recv()
            if p >= half:
                pass_on(a, p, 3, xr, left).start()
            pass_on(a, p, 5, xr, partner).start()
    for p in range(PIECES):
        for a in range(2):
            landed(a, p, 3, xo, c).wait_recv()
            pass_on(a, p, 6, xo, partner).start()
    for p in range(PIECES):
        for a in range(2):
            for kind, block in ((2, x), (4, xl), (5, xr), (6, xo)):
                landed(a, p, kind, block, 1 - c).wait_recv()
            own(a, p, 0, right).wait_send()
            own(a, p, 1, left).wait_send()
            own(a, p, 2, partner).wait_send()
            if p < half:
                pass_on(a, p, 3, xl, right).wait_send()
            else:
                pass_on(a, p, 3, xr, left).wait_send()
            pass_on(a, p, 4, xl, partner).wait_send()
            pass_on(a, p, 5, xr, partner).wait_send()
            pass_on(a, p, 6, xo, partner).wait_send()
    for a in range(2):
        keep(a).wait()


def gather(chips, lat, rope):
    rows = lat.shape[0]
    return pl.pallas_call(
        functools.partial(gather_kernel, chips),
        out_shape=[jax.ShapeDtypeStruct((rows, 2, chips) + lat.shape[1:], lat.dtype),
                   jax.ShapeDtypeStruct((rows, 2, chips) + rope.shape[1:], rope.dtype)],
        in_specs=[pl.BlockSpec(memory_space=pltpu.VMEM)] * 2,
        out_specs=[pl.BlockSpec(memory_space=pl.ANY)] * 2,
        scratch_shapes=[pltpu.SemaphoreType.DMA((2, PIECES, 7)), pltpu.SemaphoreType.DMA((2, PIECES, 7)),
                        pltpu.SemaphoreType.DMA((2,))],
        compiler_params=pltpu.CompilerParams(collective_id=0, has_side_effects=True),
        name="gather_queries",
    )(lat, rope)


def expand(ml):
    col = jnp.transpose(jnp.broadcast_to(ml[0:1, :], (128, 128)))
    return col[0:64, :], col[64:128, :]


def compact(m, l):
    return jnp.transpose(jnp.concatenate([m, l], axis=0))[0:8, :]


def attend_kernel(chips, rows, scale, lens_ref, lat_ref, rope_ref, ckv_ref, kr_ref, out_ref,
                  s_buf, p_buf, away_o, away_ml, home_o, home_ml, d2d_o, d2d_ml, one_o, one_ml, two_o, two_ml,
                  send, recv):
    x, c, xr, xl, right, left, partner = place(chips)
    xo = lax.rem(x + 2, chips)
    i = pl.program_id(0)
    local_len = ckv_ref.shape[1]
    width = ckv_ref.shape[2]
    nq = lat_ref.shape[2]
    gq = nq // chips
    hq = gq // 2
    heads = gq // 4
    k2 = scale * LOG2E
    lanes = [pl.ds(j * 128, 128) for j in range(width // 128)]

    def moves(r):
        return (
            (away_o.at[r], d2d_o.at[r], partner),
            (away_ml.at[r], d2d_ml.at[r], partner),
            (home_o.at[r, xo, pl.ds(0, hq)], one_o.at[r, 0], right),
            (home_ml.at[r, xo], one_ml.at[r, 0], right),
            (home_o.at[r, xo, pl.ds(hq, hq)], one_o.at[r, 1], left),
            (home_ml.at[r, xo], one_ml.at[r, 1], left),
            (home_o.at[r, xr], two_o.at[r, 0], right),
            (home_ml.at[r, xr], two_ml.at[r, 0], right),
            (home_o.at[r, xl], two_o.at[r, 1], left),
            (home_ml.at[r, xl], two_ml.at[r, 1], left),
        )

    def copy(r, kind):
        src, dst, dev = moves(r)[kind]
        return remote(src, dst, send.at[r, kind], recv.at[r, kind], dev)

    @pl.when(i == 0)
    def _():
        greet((right, left, partner))

    @pl.when(i < rows)
    def _():
        base = (2 * x + c) * local_len
        seen = lens_ref[jnp.minimum(i, rows - 1)] - base
        col = lax.broadcasted_iota(jnp.int32, (nq, local_len), 1)
        tok = lax.rem(lax.broadcasted_iota(jnp.int32, (nq, local_len), 0), gq) // heads
        visible = col - tok <= seen
        contract = (((1,), (1,)), ((), ()))

        def scores(n, block):
            packed = rope_ref[0, block]
            part = packed.shape[0] // chips
            rope = jnp.concatenate(
                [packed[g * part:(g + 1) * part, h * 64:(h + 1) * 64] for g in range(chips) for h in range(2)], axis=0)
            s = lax.dot_general(lat_ref[0, block], ckv_ref[0], contract, preferred_element_type=jnp.float32)
            s = s + jnp.dot(rope, kr_ref[0], preferred_element_type=jnp.float32)
            s_buf[n] = jnp.where(visible, s, MASK_FILL)

        def weigh(n):
            s = s_buf[n]
            m = jnp.max(s, axis=1, keepdims=True)
            p = jnp.exp2((s - m) * k2)
            l = jnp.sum(p, axis=1, keepdims=True)
            p_buf[n] = p.astype(jnp.bfloat16)
            return m, l

        def mix(n, m, l, o_ref, ml_ref):
            o = jnp.dot(p_buf[n], ckv_ref[0], preferred_element_type=jnp.float32)
            m = jnp.broadcast_to(m, (nq, 128))
            l = jnp.broadcast_to(l, (nq, 128))
            for g in range(chips):
                at = slice(g * gq, (g + 1) * gq)
                o_ref[i, g] = o[at]
                ml_ref[i, g] = compact(m[at], l[at])

        scores(0, 1 - c)
        scores(1, c)
        ml0 = weigh(0)
        mix(0, *ml0, away_o, away_ml)
        copy(i, 0).start()
        copy(i, 1).start()
        ml1 = weigh(1)
        mix(1, *ml1, home_o, home_ml)

    @pl.when((i >= LAG_B) & (i < rows + LAG_B))
    def _():
        r = i - LAG_B
        copy(r, 0).wait_recv()
        copy(r, 1).wait_recv()
        for g in range(chips):
            ma, la = expand(home_ml[r, g])
            mb, lb = expand(d2d_ml[r, g])
            m = jnp.maximum(ma, mb)
            fa, fb = jnp.exp2((ma - m) * k2), jnp.exp2((mb - m) * k2)
            for at in lanes:
                home_o[r, g, :, at] = home_o[r, g, :, at] * fa + d2d_o[r, g, :, at] * fb
            home_ml[r, g] = compact(m, la * fa + lb * fb)
        for kind in range(2, 6):
            copy(r, kind).start()

    @pl.when((i >= LAG_C) & (i < rows + LAG_C))
    def _():
        r = i - LAG_C
        for kind in range(2, 6):
            copy(r, kind).wait_recv()
        for side, g in ((0, xr), (1, xl)):
            part = slice(side * hq, (side + 1) * hq)
            ma, la = expand(home_ml[r, g])
            mb, lb = expand(one_ml[r, side])
            m = jnp.maximum(ma, mb)[part]
            fa, fb = jnp.exp2((ma[part] - m) * k2), jnp.exp2((mb[part] - m) * k2)
            for at in lanes:
                home_o[r, g, pl.ds(side * hq, hq), at] = (home_o[r, g, pl.ds(side * hq, hq), at] * fa
                                                          + one_o[r, side, :, at] * fb)
            l = la[part] * fa + lb[part] * fb
            if side == 0:
                m, l = jnp.concatenate([m, ma[hq:]], axis=0), jnp.concatenate([l, la[hq:]], axis=0)
            else:
                m, l = jnp.concatenate([ma[:hq], m], axis=0), jnp.concatenate([la[:hq], l], axis=0)
            home_ml[r, g] = compact(m, l)
        for kind in range(6, 10):
            copy(r, kind).start()

    @pl.when(i >= LAG_D)
    def _():
        r = i - LAG_D
        for kind in range(6, 10):
            copy(r, kind).wait_recv()
        ma, la = expand(home_ml[r, x])
        mb, lb = expand(two_ml[r, 0])
        mc, lc = expand(two_ml[r, 1])
        m = jnp.maximum(ma, jnp.maximum(mb, mc))
        fa, fb, fc = jnp.exp2((ma - m) * k2), jnp.exp2((mb - m) * k2), jnp.exp2((mc - m) * k2)
        l = la * fa + lb * fb + lc * fc
        for at in lanes:
            o = home_o[r, x, :, at] * fa + two_o[r, 0, :, at] * fb + two_o[r, 1, :, at] * fc
            out_ref[0, :, at] = (o / l).astype(out_ref.dtype)

    @pl.when(i == rows + LAG_D - 1)
    def _():
        @pl.loop(0, rows)
        def _(r):
            for kind in range(10):
                copy(r, kind).wait_send()


def attend(chips, scale, lens, lat, rope, ckv, kr):
    rows, _, nq, width = lat.shape
    gq = nq // chips
    local_len = ckv.shape[1]
    row = lambda i: jnp.minimum(i, rows - 1)
    f32, bf16 = jnp.float32, jnp.bfloat16
    return pl.pallas_call(
        functools.partial(attend_kernel, chips, rows, scale),
        grid=(rows + LAG_D,),
        out_shape=jax.ShapeDtypeStruct((rows, gq, width), bf16),
        in_specs=[pl.BlockSpec(memory_space=pltpu.SMEM),
                  pl.BlockSpec((1,) + lat.shape[1:], lambda i: (row(i), 0, 0, 0)),
                  pl.BlockSpec((1,) + rope.shape[1:], lambda i: (row(i), 0, 0, 0)),
                  pl.BlockSpec((1,) + ckv.shape[1:], lambda i: (row(i), 0, 0)),
                  pl.BlockSpec((1,) + kr.shape[1:], lambda i: (row(i), 0, 0))],
        out_specs=pl.BlockSpec((1, gq, width), lambda i: (jnp.maximum(i - LAG_D, 0), 0, 0)),
        scratch_shapes=[
            pltpu.VMEM((2, nq, local_len), f32), pltpu.VMEM((2, nq, local_len), bf16),
            pltpu.VMEM((rows, chips, gq, width), f32), pltpu.VMEM((rows, chips, 8, 128), f32),
            pltpu.VMEM((rows, chips, gq, width), f32), pltpu.VMEM((rows, chips, 8, 128), f32),
            pltpu.VMEM((rows, chips, gq, width), f32), pltpu.VMEM((rows, chips, 8, 128), f32),
            pltpu.VMEM((rows, 2, gq // 2, width), f32), pltpu.VMEM((rows, 2, 8, 128), f32),
            pltpu.VMEM((rows, 2, gq, width), f32), pltpu.VMEM((rows, 2, 8, 128), f32),
            pltpu.SemaphoreType.DMA((rows, 10)), pltpu.SemaphoreType.DMA((rows, 10))],
        compiler_params=pltpu.CompilerParams(collective_id=1, has_side_effects=True,
                                             dimension_semantics=("arbitrary",), vmem_limit_bytes=67_000_000),
        name="attend_merge",
    )(lens, lat, rope, ckv, kr)


def output_kernel(chips, ov_ref, hid_ref, w_ref, out_ref, w_buf, away, near, home, far,
                  w_sem, send, recv):
    x, c, xr, xl, right, left, partner = place(chips)
    me = 2 * x + c
    xo = lax.rem(x + 2, chips)
    cols = w_buf.shape[2]
    span = lambda dev: pl.ds(pl.multiple_of(dev * cols, 128), cols)
    dests = (xo, xr, xl, x)

    def load(k, first):
        core = 1 - c if first else c
        n = 2 * k + (0 if first else 1)
        return pltpu.make_async_copy(w_ref.at[:, span(2 * dests[k] + core)], w_buf.at[n], w_sem.at[n])

    for k in range(chips):
        load(k, True).start()
        load(k, False).start()
    peers = tuple(2 * d + c for d in dests[:3])
    greet(peers + (partner,))

    def swap(k):
        return remote(away.at[k], near.at[k], send.at[0, k], recv.at[0, k], partner)

    def reduce(k):
        return remote(home.at[k], far.at[k], send.at[1, k], recv.at[1, k], peers[k])

    for k in range(chips):
        load(k, True).wait()
        away[k] = jnp.dot(ov_ref[...], w_buf[2 * k], preferred_element_type=jnp.float32)
        swap(k).start()
        load(k, False).wait()
        home[k] = jnp.dot(ov_ref[...], w_buf[2 * k + 1], preferred_element_type=jnp.float32)
        swap(k).wait_recv()
        home[k] = home[k] + near[k]
        if k < chips - 1:
            reduce(k).start()
    for k in range(chips - 1):
        reduce(k).wait_recv()
    y = home[chips - 1] + far[0] + far[1] + far[2]
    out_ref[:, span(me)] = (hid_ref[...].astype(jnp.float32) + y).astype(out_ref.dtype)

    def spread(k):
        return remote(out_ref.at[:, span(me)], out_ref.at[:, span(me)], send.at[2, k], recv.at[2, k], peers[k])

    def mirror(k):
        ref = out_ref.at[:, span(2 * dests[k] + c)]
        return remote(ref, ref, send.at[3, k], recv.at[3, k], partner)

    def landed(kind, k, dev):
        ref = out_ref.at[:, span(dev)]
        return remote(ref, ref, send.at[kind, k], recv.at[kind, k], partner)

    for k in range(chips - 1):
        spread(k).start()
    mirror(3).start()
    source = (xo, xl, xr)
    slot = (0, 2, 1)
    for k in (1, 2, 0):
        landed(2, k, 2 * source[k] + c).wait_recv()
        mirror(slot[k]).start()
    for k in range(chips):
        landed(3, k, 2 * ((xo, xr, xl, x)[k]) + 1 - c).wait_recv()
    for k in range(chips):
        swap(k).wait_send()
        mirror(k).wait_send()
        if k < chips - 1:
            reduce(k).wait_send()
            spread(k).wait_send()


def output(chips, o_val, hidden, w_o):
    tokens, depth = o_val.shape
    dim = w_o.shape[1]
    cols = dim // (2 * chips)
    f32 = jnp.float32
    vmem = pl.BlockSpec(memory_space=pltpu.VMEM)
    return pl.pallas_call(
        functools.partial(output_kernel, chips),
        out_shape=jax.ShapeDtypeStruct((tokens, dim), hidden.dtype),
        in_specs=[vmem, vmem, pl.BlockSpec(memory_space=pl.ANY)],
        out_specs=vmem,
        scratch_shapes=[
            pltpu.VMEM((2 * chips, depth, cols), w_o.dtype),
            pltpu.VMEM((chips, tokens, cols), f32), pltpu.VMEM((chips, tokens, cols), f32),
            pltpu.VMEM((chips, tokens, cols), f32), pltpu.VMEM((chips - 1, tokens, cols), f32),
            pltpu.SemaphoreType.DMA((2 * chips,)),
            pltpu.SemaphoreType.DMA((4, chips)), pltpu.SemaphoreType.DMA((4, chips))],
        compiler_params=pltpu.CompilerParams(collective_id=2, has_side_effects=True, vmem_limit_bytes=60_000_000),
        name="project_output",
    )(o_val, hidden, w_o)


def solution(mesh):
    chips = mesh.shape["seq"] // 2

    def local_step(hidden, cache_lens, c_kv, k_r, w_uq, w_qr, w_uk, w_uv, w_o):
        rows, toks, dim = hidden.shape
        heads, nope, width = w_uk.shape
        rope_dim = w_qr.shape[2]
        value = w_uv.shape[2]
        score_scale = (nope + rope_dim) ** -0.5
        f32, bf16 = jnp.float32, jnp.bfloat16
        q_nope = jnp.einsum("cre,eil->cril", hidden, w_uq, preferred_element_type=f32).astype(bf16)
        q_rope = jnp.einsum("cre,eis->cris", hidden, w_qr, preferred_element_type=f32).astype(bf16)
        q_lat = jnp.einsum("bqhk,hkc->bqhc", q_nope, w_uk, preferred_element_type=f32).astype(bf16)
        gq = toks * heads
        packed = q_rope.reshape(rows, 2, gq // 2, rope_dim).transpose(0, 2, 1, 3).reshape(rows, gq // 2, 2 * rope_dim)
        lat_all, rope_all = gather(chips, q_lat.reshape(rows, gq, width), packed)
        o_lat = attend(chips, score_scale, cache_lens,
                       lat_all.reshape(rows, 2, chips * gq, width),
                       rope_all.reshape(rows, 2, chips * gq // 2, 2 * rope_dim), c_kv, jnp.swapaxes(k_r, 1, 2))
        o_val = jnp.einsum("bqhc,hcv->bqhv", o_lat.reshape(rows, toks, heads, width), w_uv,
                           preferred_element_type=f32).astype(bf16)
        cols = dim // (2 * chips)
        own = lax.dynamic_slice_in_dim(hidden, lax.axis_index("seq") * cols, cols, axis=2)
        out = output(chips, o_val.reshape(rows * toks, heads * value), own.reshape(rows * toks, cols),
                     w_o.reshape(heads * value, dim))
        return out.reshape(rows, toks, dim)

    specs_in = (P("batch", None, None), P("batch"), P("batch", "seq", None), P("batch", "seq", None),
                P(None, "seq", None), P(None, "seq", None), P("seq", None, None), P("seq", None, None),
                P("seq", None, None))
    return jax.shard_map(local_step, mesh=mesh, in_specs=specs_in, out_specs=P("batch", None, None), check_vma=False)
```

time: 410 us -> 210 us (0.51)
  Pallas kernels: 0 us -> 174 us
  waiting for transfers between devices: 170 us -> 0 us
  matrix products: 170 us -> 28.6 us
  other arithmetic: 25.4 us -> 0 us
  blocking collectives: 20.9 us -> 0 us
  between operations: 13.3 us -> 0.08 us
    pallas_call x0 -> x3, Pallas kernels: none -> 174 us  [the longest x1 98.2 us: attend(): pl.pallas_call(functools.partial(attend_kernel, chips, rows, scale), grid...]
    dot_general x7 -> x4, matrix products: 170 us -> 28.6 us  [the longest x1 14.7 us: local_step(): jnp.einsum('cre,eil->cril', hidden, w_uq, preferred_element_type=f32)]
    reduce_scatter x1 -> x0, waiting for transfers between devices: 88 us -> none  [local_step(): lax.psum_scatter(o_part * rescale[..., None], 'seq', scatter_dimension=2,...]
    psum x1 -> x0, waiting for transfers between devices: 54.9 us -> none  [local_step(): y_sum = lax.psum(y_part, 'seq')]
    all_gather x2 -> x0, waiting for transfers between devices: 26.7 us -> none  [the longest x1 22.3 us: local_step(): lat_all = lax.all_gather(q_lat, 'seq', axis=2, tiled=True)]
    reduce_sum x1 -> x0, other arithmetic: 21.1 us -> none  [local_step(): local_sum = jnp.sum(weights, axis=-1)]
    pmax x1 -> x0, blocking collectives: 20.9 us -> none  [local_step(): global_max = lax.pmax(local_max, 'seq')]
    reshape x0 -> x4, local copies, waits for them, and re-layouts: none -> 4.29 us  [the longest x1 2.52 us: local_step(): return out.reshape(rows, toks, dim)]
  transfers between devices with their start and end apart: 5 -> 0, of which waited for: 4 -> 0; matrix products, arithmetic and copies ran while one was open for 22% -> 0% of each run, Pallas kernels for 0% -> 0%
where the time goes in v1:
time: 210 us
  Pallas kernels  174 us (83%)
  matrix products  28.6 us (14%)
  local copies, waits for them, and re-layouts  7.72 us (4%)
    pallas_call x1, Pallas kernels, attend(): pl.pallas_call(functools.partial(attend_kernel, chips, rows, scale), grid...  98.2 us
    pallas_call x1, Pallas kernels, gather(): pl.pallas_call(functools.partial(gather_kernel, chips), out_shape=[jax.Sh...  47.6 us
    pallas_call x1, Pallas kernels, output(): pl.pallas_call(functools.partial(output_kernel, chips), out_shape=jax.Sha...  28.1 us
    dot_general x1, matrix products, local_step(): jnp.einsum('cre,eil->cril', hidden, w_uq, preferred_element_type=f32)  14.7 us
    dot_general x1, matrix products, local_step(): jnp.einsum('cre,eis->cris', hidden, w_qr, preferred_element_type=f32)  10.3 us

profile of v1, /device:TPU:113, one launch (start us, length us, event | category | flops | bytes accessed | tf_op | source)
XLA Modules:
  0.0 210.3 jit_solution(11752425906196777398)
XLA Ops:
  0.0 0.0 copy-start
  0.0 0.0 copy-start.1
  0.0 14.7 %fusion.20 = bf16[16,4,16,128]{3,0,1,2:T(8,128)(2,1)S(1)} fusion(bf16[7168,16,128,1]{2,1,0,3:T(8,128)(2,1)} %bitcast.58, bf16[16,4,7168,1]{2,1,0,3:T(4,128)(2,1)} %bitcast.56), kind=kOutput, calls=%fused_computation.12 | convolution fusion | flops 1879179264 | bytes 30539776 | tf_op jit(solution)/shard_map/cre,eil->cril/dot_general | solution.py:401
  14.7 0.0 copy-done
  14.7 0.4 fusion.11
  15.1 1.5 copy.10
  16.7 0.0 copy-done.1
  16.7 10.3 %fusion.17 = bf16[16,4,16,64]{3,0,2,1:T(8,128)(2,1)S(1)} fusion(bf16[7168,16,64]{0,2,1:T(8,128)(2,1)} %param.14, bf16[16,4,7168,1]{2,1,0,3:T(4,128)(2,1)S(1)} %bitcast.57), kind=kOutput, calls=%fused_computation.11 | convolution fusion | flops 939589632 | bytes 15728640 | tf_op jit(solution)/shard_map/cre,eis->cris/dot_general | solution.py:402
  27.0 0.3 copy.36
  27.2 0.8 reshape.32.rope_ref
  28.0 47.6 %gather_queries.1 = (bf16[16,2,4,64,512]{4,3,2,1,0:T(8,128)(2,1)}, bf16[16,2,4,32,128]{4,3,2,1,0:T(8,128)(2,1)}) custom-call(bf16[16,64,512]{2,1,0:T(8,128)(2,1)} %bitcast.50, bf16[16,32,128]{2,1,0:T(8,128)(2,1)} %reshape.32.rope_ref), custom_call_target="tpu_custom_call" | custom-call | tf_op jit(solution)/shard_map/gather_queries/pallas_call | solution.py:104
  75.7 98.2 %attend_merge.1 = bf16[16,64,512]{2,1,0:T(8,128)(2,1)} custom-call(s32[16]{0:T(128)} %lens_ref.1, bf16[16,2,256,512]{3,2,1,0:T(8,128)(2,1)} %bitcast.47, bf16[16,2,128,128]{3,2,1,0:T(8,128)(2,1)} %bitcast.52, bf16[16,2048,512]{2,1,0:T(8,128)(2,1)} %ckv_ref.1, bf16[16,64,2048]{2,1,0:T(8,128)(2,1)} %bitcast.48), custom_call_target="tpu_custom_call" | custom-call | tf_op jit(solution)/shard_map/attend_merge/pallas_call | solution.py:275
  173.9 3.2 %fusion.23 = bf16[16,4,16,128]{3,0,1,2:T(8,128)(2,1)S(1)} fusion(bf16[16,512,128]{2,1,0:T(8,128)(2,1)} %param.16, bf16[16,4,16,512]{3,2,1,0:T(8,128)(2,1)} %bitcast.49), kind=kOutput, calls=%fused_computation.13 | convolution fusion | flops 134348800 | bytes 3407872 | tf_op jit(solution)/shard_map/bqhc,hcv->bqhv/dot_general | solution.py:410
  177.1 0.2 copy.14
  177.3 0.8 copy.35
  178.1 0.9 constant_dynamic-slice_fusion
  179.0 0.7 reshape.37.hid_ref
  179.7 28.1 %project_output.1 = bf16[64,7168]{1,0:T(8,128)(2,1)} custom-call(bf16[64,2048]{1,0:T(8,128)(2,1)} %bitcast.51, bf16[64,896]{1,0:T(8,128)(2,1)} %reshape.37.hid_ref, bf16[2048,7168]{1,0:T(8,128)(2,1)} %bitcast.46), custom_call_target="tpu_custom_call" | custom-call | tf_op jit(solution)/shard_map/project_output/pallas_call | solution.py:375
  207.8 2.5 %reshape.39 = bf16[16,4,7168]{2,1,0:T(4,128)(2,1)} reshape(bf16[64,7168]{1,0:T(8,128)(2,1)} %project_output.1) | data formatting | bytes 1835008 | tf_op jit(solution)/shard_map/reshape | solution.py:416
Async XLA Ops:
  0.0 14.7 %copy-start = (bf16[16,128,512]{2,1,0:T(8,128)(2,1)S(1)}, bf16[16,128,512]{2,1,0:T(8,128)(2,1)}, u32[]{:S(2)}) copy-start(bf16[16,128,512]{2,1,0:T(8,128)(2,1)} %param.15) | copy-start | bytes 6291460
  0.0 16.7 %copy-start.1 = (bf16[16,4,7168]{2,1,0:T(4,128)(2,1)S(1)}, bf16[16,4,7168]{2,1,0:T(4,128)(2,1)}, u32[]{:S(2)}) copy-start(bf16[16,4,7168]{2,1,0:T(4,128)(2,1)} %param.9) | copy-start | bytes 2752516

commit v2 on v1

--- a/solution.py
+++ b/solution.py
@@ -10,8 +10,8 @@
 MASK_FILL = -1e30
 LOG2E = 1.4426950408889634
 MESH = pl.DeviceIdType.MESH
-LAG_B, LAG_C, LAG_D = 1, 3, 5
-PIECES = 4
+LAG_B, LAG_C, LAG_D = 2, 4, 7
+CUTS = 4
 
 
 def remote(src, dst, send_sem, recv_sem, dev):
@@ -33,85 +33,184 @@
     pl.semaphore_wait(barrier, len(devs))
 
 
-def gather_kernel(chips, lat_ref, rope_ref, lat_all, rope_all, send, recv, local):
+def pack(vals, dst, slot):
+    n = vals[0].shape[0]
+    low = lax.rem(lax.broadcasted_iota(jnp.int32, vals[0].shape, 0), 8) < 4
+    even = [jnp.where(low, p, pltpu.roll(q, 4, 0)) for p, q in (vals[:2], vals[2:])]
+    odd = [jnp.where(low, pltpu.roll(p, n - 4, 0), q) for p, q in (vals[:2], vals[2:])]
+    for v in range(n // 8):
+        at = slice(8 * v, 8 * v + 8)
+        for side, both in ((0, even), (1, odd)):
+            dst[2 * v + side, pl.ds(slot, 16)] = jnp.concatenate([both[0][at], both[1][at]], axis=0).astype(dst.dtype)
+
+
+def query_kernel(chips, hid_ref, wq_ref, wr_ref, wk_ref, lat_all, rope_all,
+                 wq_buf, wr_buf, wk_buf, wide, acc, lat_own, rope_own, wq_sem, wr_sem, wk_sem, send, recv, local):
     x, c, xr, xl, right, left, partner = place(chips)
     xo = lax.rem(x + 2, chips)
-    step = lat_ref.shape[0] // PIECES
-    pairs = ((lat_ref, lat_all), (rope_ref, rope_all))
-    half = PIECES // 2
-    greet((right, left, partner))
-    rows = lambda p: pl.ds(p * step, step)
-
-    def copy(a, p, kind, src, slot, dev):
-        return remote(src, pairs[a][1].at[rows(p), slot[1], slot[0]], send.at[a, p, kind], recv.at[a, p, kind], dev)
-
-    def own(a, p, kind, dev):
-        return copy(a, p, kind, pairs[a][0].at[rows(p)], (x, c), dev)
-
-    def pass_on(a, p, kind, block, dev):
-        return copy(a, p, kind, pairs[a][1].at[rows(p), c, block], (block, c), dev)
-
-    def landed(a, p, kind, block, core):
-        ref = pairs[a][1].at[rows(p), core, block]
-        return remote(ref, ref, send.at[a, p, kind], recv.at[a, p, kind], partner)
-
-    keep = lambda a: pltpu.make_async_copy(pairs[a][0], pairs[a][1].at[:, c, x], local.at[a])
-    order_l = [(p + half) % PIECES for p in range(PIECES)]
-    for i in range(PIECES):
-        for a in range(2):
-            own(a, i, 0, right).start()
-            own(a, order_l[i], 1, left).start()
-    for p in range(PIECES):
-        for a in range(2):
-            own(a, p, 2, partner).start()
-    for a in range(2):
-        keep(a).start()
-    for i in range(PIECES):
-        for a in range(2):
-            landed(a, i, 0, xl, c).wait_recv()
-            if i < half:
-                pass_on(a, i, 3, xl, right).start()
-            pass_on(a, i, 4, xl, partner).start()
-            p = order_l[i]
-            landed(a, p, 1, xr, c).wait_recv()
-            if p >= half:
-                pass_on(a, p, 3, xr, left).start()
-            pass_on(a, p, 5, xr, partner).start()
-    for p in range(PIECES):
-        for a in range(2):
-            landed(a, p, 3, xo, c).wait_recv()
-            pass_on(a, p, 6, xo, partner).start()
-    for p in range(PIECES):
-        for a in range(2):
-            for kind, block in ((2, x), (4, xl), (5, xr), (6, xo)):
-                landed(a, p, kind, block, 1 - c).wait_recv()
-            own(a, p, 0, right).wait_send()
-            own(a, p, 1, left).wait_send()
-            own(a, p, 2, partner).wait_send()
-            if p < half:
-                pass_on(a, p, 3, xl, right).wait_send()
+    rows, toks, dim = hid_ref.shape
+    pairs, nope = wq_ref.shape[1], wq_ref.shape[3]
+    per_ch = pairs // 2
+    depth = dim // CUTS
+    f32, bf16 = jnp.float32, jnp.bfloat16
+
+    barrier = pltpu.get_barrier_semaphore()
+    for dev in (right, left, partner):
+        pl.semaphore_signal(barrier, inc=1, device_id={"seq": dev}, device_id_type=MESH)
+
+    def load(u, k):
+        return pltpu.make_async_copy(wq_ref.at[pl.ds(k * depth, depth), u], wq_buf.at[u, pl.ds(k * depth, depth)],
+                                     wq_sem.at[u, k])
+
+    def load_rope(k):
+        n = wr_ref.shape[0] // CUTS
+        return pltpu.make_async_copy(wr_ref.at[pl.ds(k * n, n)], wr_buf.at[pl.ds(k * n, n)], wr_sem.at[k])
+
+    load_up = pltpu.make_async_copy(wk_ref, wk_buf, wk_sem)
+    for k in range(CUTS):
+        for u in range(per_ch):
+            load(u, k).start()
+    load_up.start()
+
+    lane = lax.broadcasted_iota(jnp.int32, (128, 512), 1)
+    src = lax.broadcasted_iota(jnp.int32, (128, 512), 0)
+    spread = jnp.where(lax.rem(lane, 256) == 2 * src + lane // 256, 1.0, 0.0).astype(bf16)
+    tiles = depth // 128
+    n = rows * toks
+    for k in range(CUTS):
+        stack = jnp.concatenate([hid_ref[:, :, (k * tiles + t) * 128:(k * tiles + t + 1) * 128].reshape(n, 128)
+                                 for t in range(tiles)], axis=0)
+        res = jnp.dot(stack, spread, preferred_element_type=f32).astype(bf16)
+        for t in range(tiles):
+            for side in range(2):
+                wide[k, pl.ds(side * n, n), pl.ds(t * 256, 256)] = res[t * n:(t + 1) * n, side * 256:side * 256 + 256]
+
+    where = lambda p: pl.ds((p % 2) * 2 * 16 + (p // 2) * 16, 16) if p < 4 else pl.ds((p - 4) * 16, 16)
+    own_ref = lambda p: (lat_own if p < 4 else rope_own).at[:, where(p)]
+    all_ref = lambda p, core, block: (lat_all if p < 4 else rope_all).at[:, core, block, where(p)]
+
+    def own(p, kind, dev):
+        return remote(own_ref(p), all_ref(p, c, x), send.at[p, kind], recv.at[p, kind], dev)
+
+    def pass_on(p, kind, block, dev):
+        return remote(all_ref(p, c, block), all_ref(p, c, block), send.at[p, kind], recv.at[p, kind], dev)
+
+    def landed(p, kind, block, core):
+        ref = all_ref(p, core, block)
+        return remote(ref, ref, send.at[p, kind], recv.at[p, kind], partner)
+
+    keep = lambda p: pltpu.make_async_copy(own_ref(p), all_ref(p, c, x), local.at[p])
+
+    def send_own(p):
+        own(p, 0, right).start()
+        own(p + 1, 0, right).start()
+        own(p + 1, 1, left).start()
+        own(p, 1, left).start()
+        for q in (p, p + 1):
+            own(q, 2, partner).start()
+            keep(q).start()
+
+    def relay(p):
+        landed(p, 0, xl, c).wait_recv()
+        pass_on(p, 3, xl, right).start()
+        pass_on(p, 4, xl, partner).start()
+        landed(p + 1, 1, xr, c).wait_recv()
+        pass_on(p + 1, 3, xr, left).start()
+        pass_on(p + 1, 5, xr, partner).start()
+        landed(p + 1, 0, xl, c).wait_recv()
+        pass_on(p + 1, 4, xl, partner).start()
+        landed(p, 1, xr, c).wait_recv()
+        pass_on(p, 5, xr, partner).start()
+
+    for ch in range(2):
+        base = ch * per_ch
+        acc[...] = jnp.zeros_like(acc)
+
+        @pl.loop(0, CUTS)
+        def _(k):
+            for u in range(base, base + per_ch):
+                load(u, k).wait()
+            if ch == 0:
+                for u in range(per_ch, pairs):
+                    load(u, k).start()
             else:
-                pass_on(a, p, 3, xr, left).wait_send()
-            pass_on(a, p, 4, xl, partner).wait_send()
-            pass_on(a, p, 5, xr, partner).wait_send()
-            pass_on(a, p, 6, xo, partner).wait_send()
-    for a in range(2):
-        keep(a).wait()
-
-
-def gather(chips, lat, rope):
-    rows = lat.shape[0]
+                load_rope(k).start()
+            for j in range(per_ch // 2):
+                w = [wq_buf[base + 2 * j + h, pl.ds(k * depth, depth)].reshape(2 * depth, nope) for h in range(2)]
+                acc[j] += jnp.dot(wide[k], jnp.concatenate(w, axis=1), preferred_element_type=f32)
+
+        if ch == 0:
+            load_up.wait()
+        for side in range(2):
+            q_lat = []
+            for u in range(per_ch):
+                q_n = acc[u // 2, pl.ds(side * n, n), pl.ds((u % 2) * nope, nope)].astype(bf16)
+                q_lat.append(jnp.dot(q_n, wk_buf[2 * (base + u) + side], preferred_element_type=f32))
+            pack(q_lat, lat_own, side * 32 + ch * 16)
+        if ch == 0:
+            pl.semaphore_wait(barrier, 3)
+        send_own(2 * ch)
+    relay(0)
+
+    tokens = jnp.concatenate([hid_ref[:, :, t * 128:(t + 1) * 128].reshape(n, 128) for t in range(dim // 128)], axis=1)
+    part = wr_buf.shape[0] // CUTS
+    q_rope = []
+    for k in range(CUTS):
+        load_rope(k).wait()
+        r = lax.dot_general(tokens, wr_buf[pl.ds(k * part, part)], (((1,), (1,)), ((), ())), preferred_element_type=f32)
+        q_rope += [r[:, j * 128:(j + 1) * 128] for j in range(part // 128)]
+    for h in range(2):
+        pack(q_rope[4 * h:4 * h + 4], rope_own, 16 * h)
+    send_own(4)
+    relay(2)
+    relay(4)
+    for p in range(6):
+        landed(p, 3, xo, c).wait_recv()
+        pass_on(p, 6, xo, partner).start()
+    for p in range(6):
+        for kind, block in ((2, x), (4, xl), (5, xr), (6, xo)):
+            landed(p, kind, block, 1 - c).wait_recv()
+        own(p, 0, right).wait_send()
+        own(p, 1, left).wait_send()
+        own(p, 2, partner).wait_send()
+        if p % 2 == 0:
+            pass_on(p, 3, xl, right).wait_send()
+        else:
+            pass_on(p, 3, xr, left).wait_send()
+        pass_on(p, 4, xl, partner).wait_send()
+        pass_on(p, 5, xr, partner).wait_send()
+        pass_on(p, 6, xo, partner).wait_send()
+        keep(p).wait()
+
+
+def queries(chips, hidden, w_uq, w_qr, w_uk):
+    rows, toks, dim = hidden.shape
+    heads, nope, width = w_uk.shape
+    gq = heads * toks
+    bf16 = jnp.bfloat16
+    wq = w_uq.reshape(dim, heads // 2, 2, nope)
+    wr = jnp.transpose(w_qr, (1, 2, 0)).reshape(-1, dim)
+    hbm = pl.BlockSpec(memory_space=pl.ANY)
+    dma = pltpu.SemaphoreType.DMA
     return pl.pallas_call(
-        functools.partial(gather_kernel, chips),
-        out_shape=[jax.ShapeDtypeStruct((rows, 2, chips) + lat.shape[1:], lat.dtype),
-                   jax.ShapeDtypeStruct((rows, 2, chips) + rope.shape[1:], rope.dtype)],
-        in_specs=[pl.BlockSpec(memory_space=pltpu.VMEM)] * 2,
-        out_specs=[pl.BlockSpec(memory_space=pl.ANY)] * 2,
-        scratch_shapes=[pltpu.SemaphoreType.DMA((2, PIECES, 7)), pltpu.SemaphoreType.DMA((2, PIECES, 7)),
-                        pltpu.SemaphoreType.DMA((2,))],
-        compiler_params=pltpu.CompilerParams(collective_id=0, has_side_effects=True),
-        name="gather_queries",
-    )(lat, rope)
+        functools.partial(query_kernel, chips),
+        out_shape=[jax.ShapeDtypeStruct((rows, 2, chips, gq, width), bf16),
+                   jax.ShapeDtypeStruct((rows, 2, chips, gq // 2, 128), bf16)],
+        in_specs=[pl.BlockSpec(memory_space=pltpu.VMEM), hbm, hbm, hbm],
+        out_specs=[hbm] * 2,
+        scratch_shapes=[
+            pltpu.VMEM((heads // 2, dim, 2, nope), bf16), pltpu.VMEM(wr.shape, bf16), pltpu.VMEM(w_uk.shape, bf16),
+            pltpu.VMEM((CUTS, 2 * rows * toks, 2 * dim // CUTS), bf16),
+            pltpu.VMEM((heads // 8, 2 * rows * toks, 2 * nope), jnp.float32),
+            pltpu.VMEM((rows, gq, width), bf16), pltpu.VMEM((rows, gq // 2, 128), bf16),
+            dma((heads // 2, CUTS)), dma((CUTS,)), dma(()), dma((6, 7)), dma((6, 7)), dma((6,))],
+        compiler_params=pltpu.CompilerParams(collective_id=0, has_side_effects=True, vmem_limit_bytes=67_000_000),
+        name="make_queries",
+    )(hidden, wq, wr, w_uk)
+
+
+def token(row):
+    return lax.rem(row, 4)
 
 
 def expand(ml):
@@ -134,7 +233,6 @@
     nq = lat_ref.shape[2]
     gq = nq // chips
     hq = gq // 2
-    heads = gq // 4
     k2 = scale * LOG2E
     lanes = [pl.ds(j * 128, 128) for j in range(width // 128)]
 
@@ -160,55 +258,17 @@
     def _():
         greet((right, left, partner))
 
-    @pl.when(i < rows)
-    def _():
-        base = (2 * x + c) * local_len
-        seen = lens_ref[jnp.minimum(i, rows - 1)] - base
-        col = lax.broadcasted_iota(jnp.int32, (nq, local_len), 1)
-        tok = lax.rem(lax.broadcasted_iota(jnp.int32, (nq, local_len), 0), gq) // heads
-        visible = col - tok <= seen
-        contract = (((1,), (1,)), ((), ()))
-
-        def scores(n, block):
-            packed = rope_ref[0, block]
-            part = packed.shape[0] // chips
-            rope = jnp.concatenate(
-                [packed[g * part:(g + 1) * part, h * 64:(h + 1) * 64] for g in range(chips) for h in range(2)], axis=0)
-            s = lax.dot_general(lat_ref[0, block], ckv_ref[0], contract, preferred_element_type=jnp.float32)
-            s = s + jnp.dot(rope, kr_ref[0], preferred_element_type=jnp.float32)
-            s_buf[n] = jnp.where(visible, s, MASK_FILL)
-
-        def weigh(n):
-            s = s_buf[n]
-            m = jnp.max(s, axis=1, keepdims=True)
-            p = jnp.exp2((s - m) * k2)
-            l = jnp.sum(p, axis=1, keepdims=True)
-            p_buf[n] = p.astype(jnp.bfloat16)
-            return m, l
-
-        def mix(n, m, l, o_ref, ml_ref):
-            o = jnp.dot(p_buf[n], ckv_ref[0], preferred_element_type=jnp.float32)
-            m = jnp.broadcast_to(m, (nq, 128))
-            l = jnp.broadcast_to(l, (nq, 128))
-            for g in range(chips):
-                at = slice(g * gq, (g + 1) * gq)
-                o_ref[i, g] = o[at]
-                ml_ref[i, g] = compact(m[at], l[at])
-
-        scores(0, 1 - c)
-        scores(1, c)
-        ml0 = weigh(0)
-        mix(0, *ml0, away_o, away_ml)
-        copy(i, 0).start()
-        copy(i, 1).start()
-        ml1 = weigh(1)
-        mix(1, *ml1, home_o, home_ml)
-
-    @pl.when((i >= LAG_B) & (i < rows + LAG_B))
-    def _():
-        r = i - LAG_B
-        copy(r, 0).wait_recv()
-        copy(r, 1).wait_recv()
+    def late(lag):
+        return jnp.where((i >= lag) & (i < rows + lag), i - lag, rows)
+
+    def on_row(lag, act, kinds):
+        @pl.when((i >= lag) & (i < rows + lag))
+        def _():
+            for kind in kinds:
+                act(copy(i - lag, kind))
+
+    def merge_pair():
+        r = late(LAG_B)
         for g in range(chips):
             ma, la = expand(home_ml[r, g])
             mb, lb = expand(d2d_ml[r, g])
@@ -217,14 +277,9 @@
             for at in lanes:
                 home_o[r, g, :, at] = home_o[r, g, :, at] * fa + d2d_o[r, g, :, at] * fb
             home_ml[r, g] = compact(m, la * fa + lb * fb)
-        for kind in range(2, 6):
-            copy(r, kind).start()
-
-    @pl.when((i >= LAG_C) & (i < rows + LAG_C))
-    def _():
-        r = i - LAG_C
-        for kind in range(2, 6):
-            copy(r, kind).wait_recv()
+
+    def merge_half():
+        r = late(LAG_C)
         for side, g in ((0, xr), (1, xl)):
             part = slice(side * hq, (side + 1) * hq)
             ma, la = expand(home_ml[r, g])
@@ -240,14 +295,9 @@
             else:
                 m, l = jnp.concatenate([ma[:hq], m], axis=0), jnp.concatenate([la[:hq], l], axis=0)
             home_ml[r, g] = compact(m, l)
-        for kind in range(6, 10):
-            copy(r, kind).start()
-
-    @pl.when(i >= LAG_D)
-    def _():
-        r = i - LAG_D
-        for kind in range(6, 10):
-            copy(r, kind).wait_recv()
+
+    def finish():
+        r = late(LAG_D)
         ma, la = expand(home_ml[r, x])
         mb, lb = expand(two_ml[r, 0])
         mc, lc = expand(two_ml[r, 1])
@@ -257,6 +307,65 @@
         for at in lanes:
             o = home_o[r, x, :, at] * fa + two_o[r, 0, :, at] * fb + two_o[r, 1, :, at] * fc
             out_ref[0, :, at] = (o / l).astype(out_ref.dtype)
+
+    on_row(LAG_B, lambda cp: cp.wait_recv(), range(0, 2))
+    on_row(LAG_C, lambda cp: cp.wait_recv(), range(2, 6))
+    on_row(LAG_D, lambda cp: cp.wait_recv(), range(6, 10))
+
+    @pl.when(i < rows)
+    def _():
+        base = (2 * x + c) * local_len
+        seen = lens_ref[jnp.minimum(i, rows - 1)] - base
+        col = lax.broadcasted_iota(jnp.int32, (nq, local_len), 1)
+        tok = token(lax.broadcasted_iota(jnp.int32, (nq, 1), 0))
+        visible = col <= seen + tok
+        contract = (((1,), (1,)), ((), ()))
+
+        def scores(n, block):
+            packed = rope_ref[0, block]
+            part = packed.shape[0] // chips
+            rope = jnp.concatenate(
+                [packed[g * part:(g + 1) * part, h * 64:(h + 1) * 64] for g in range(chips) for h in range(2)], axis=0)
+            s = lax.dot_general(lat_ref[0, block], ckv_ref[0], contract, preferred_element_type=jnp.float32)
+            s = s + jnp.dot(rope, kr_ref[0], preferred_element_type=jnp.float32)
+            s_buf[n] = jnp.where(visible, s, MASK_FILL)
+
+        def weigh(n):
+            s = s_buf[n]
+            m = jnp.max(s, axis=1, keepdims=True)
+            p = jnp.exp2((s - m) * k2)
+            l = jnp.sum(p, axis=1, keepdims=True)
+            p_buf[n] = p.astype(jnp.bfloat16)
+            return m, l
+
+        def mix(n, m, l, o_ref, ml_ref):
+            o = jnp.dot(p_buf[n], ckv_ref[0], preferred_element_type=jnp.float32)
+            m = jnp.broadcast_to(m, (nq, 128))
+            l = jnp.broadcast_to(l, (nq, 128))
+            for g in range(chips):
+                at = slice(g * gq, (g + 1) * gq)
+                o_ref[i, g] = o[at]
+                ml_ref[i, g] = compact(m[at], l[at])
+
+        merge_pair()
+        scores(0, 1 - c)
+        merge_half()
+        scores(1, c)
+        finish()
+        ml0 = weigh(0)
+        mix(0, *ml0, away_o, away_ml)
+        ml1 = weigh(1)
+        mix(1, *ml1, home_o, home_ml)
+
+    @pl.when(i >= rows)
+    def _():
+        merge_pair()
+        merge_half()
+        finish()
+
+    on_row(0, lambda cp: cp.start(), range(0, 2))
+    on_row(LAG_B, lambda cp: cp.start(), range(2, 6))
+    on_row(LAG_C, lambda cp: cp.start(), range(6, 10))
 
     @pl.when(i == rows + LAG_D - 1)
     def _():
@@ -284,11 +393,11 @@
         out_specs=pl.BlockSpec((1, gq, width), lambda i: (jnp.maximum(i - LAG_D, 0), 0, 0)),
         scratch_shapes=[
             pltpu.VMEM((2, nq, local_len), f32), pltpu.VMEM((2, nq, local_len), bf16),
-            pltpu.VMEM((rows, chips, gq, width), f32), pltpu.VMEM((rows, chips, 8, 128), f32),
-            pltpu.VMEM((rows, chips, gq, width), f32), pltpu.VMEM((rows, chips, 8, 128), f32),
-            pltpu.VMEM((rows, chips, gq, width), f32), pltpu.VMEM((rows, chips, 8, 128), f32),
-            pltpu.VMEM((rows, 2, gq // 2, width), f32), pltpu.VMEM((rows, 2, 8, 128), f32),
-            pltpu.VMEM((rows, 2, gq, width), f32), pltpu.VMEM((rows, 2, 8, 128), f32),
+            pltpu.VMEM((rows + 1, chips, gq, width), f32), pltpu.VMEM((rows + 1, chips, 8, 128), f32),
+            pltpu.VMEM((rows + 1, chips, gq, width), f32), pltpu.VMEM((rows + 1, chips, 8, 128), f32),
+            pltpu.VMEM((rows + 1, chips, gq, width), f32), pltpu.VMEM((rows + 1, chips, 8, 128), f32),
+            pltpu.VMEM((rows + 1, 2, gq // 2, width), f32), pltpu.VMEM((rows + 1, 2, 8, 128), f32),
+            pltpu.VMEM((rows + 1, 2, gq, width), f32), pltpu.VMEM((rows + 1, 2, 8, 128), f32),
             pltpu.SemaphoreType.DMA((rows, 10)), pltpu.SemaphoreType.DMA((rows, 10))],
         compiler_params=pltpu.CompilerParams(collective_id=1, has_side_effects=True,
                                              dimension_semantics=("arbitrary",), vmem_limit_bytes=67_000_000),
@@ -398,17 +507,13 @@
         value = w_uv.shape[2]
         score_scale = (nope + rope_dim) ** -0.5
         f32, bf16 = jnp.float32, jnp.bfloat16
-        q_nope = jnp.einsum("cre,eil->cril", hidden, w_uq, preferred_element_type=f32).astype(bf16)
-        q_rope = jnp.einsum("cre,eis->cris", hidden, w_qr, preferred_element_type=f32).astype(bf16)
-        q_lat = jnp.einsum("bqhk,hkc->bqhc", q_nope, w_uk, preferred_element_type=f32).astype(bf16)
         gq = toks * heads
-        packed = q_rope.reshape(rows, 2, gq // 2, rope_dim).transpose(0, 2, 1, 3).reshape(rows, gq // 2, 2 * rope_dim)
-        lat_all, rope_all = gather(chips, q_lat.reshape(rows, gq, width), packed)
+        lat_all, rope_all = queries(chips, hidden, w_uq, w_qr, w_uk)
         o_lat = attend(chips, score_scale, cache_lens,
                        lat_all.reshape(rows, 2, chips * gq, width),
                        rope_all.reshape(rows, 2, chips * gq // 2, 2 * rope_dim), c_kv, jnp.swapaxes(k_r, 1, 2))
-        o_val = jnp.einsum("bqhc,hcv->bqhv", o_lat.reshape(rows, toks, heads, width), w_uv,
-                           preferred_element_type=f32).astype(bf16)
+        o_val = jnp.einsum("bpuqc,upcv->bqupv", o_lat.reshape(rows, 2, heads // 2, toks, width),
+                           w_uv.reshape(heads // 2, 2, width, value), preferred_element_type=f32).astype(bf16)
         cols = dim // (2 * chips)
         own = lax.dynamic_slice_in_dim(hidden, lax.axis_index("seq") * cols, cols, axis=2)
         out = output(chips, o_val.reshape(rows * toks, heads * value), own.reshape(rows * toks, cols),

time: 210 us -> 189 us (0.900)
  matrix products: 28.6 us -> 2.39 us
  Pallas kernels: 174 us -> 180 us
    dot_general x4 -> x1, matrix products: 28.6 us -> 2.39 us  [local_step(): jnp.einsum('bpuqc,upcv->bqupv', o_lat.reshape(rows, 2, heads // 2, toks,...]
    pallas_call x1, Pallas kernels: 47.6 us -> 56.5 us  [queries(): pl.pallas_call(functools.partial(query_kernel, chips), out_shape=[jax.Sha...]
    pallas_call x1, Pallas kernels: 98.2 us -> 95.7 us  [attend(): pl.pallas_call(functools.partial(attend_kernel, chips, rows, scale), grid...]
where the time goes in v2:
time: 189 us
  Pallas kernels  180 us (95%)
  local copies, waits for them, and re-layouts  6.65 us (4%)
  matrix products  2.39 us (1%)
    pallas_call x1, Pallas kernels, attend(): pl.pallas_call(functools.partial(attend_kernel, chips, rows, scale), grid...  95.7 us
    pallas_call x1, Pallas kernels, queries(): pl.pallas_call(functools.partial(query_kernel, chips), out_shape=[jax.Sha...  56.5 us
    pallas_call x1, Pallas kernels, output(): pl.pallas_call(functools.partial(output_kernel, chips), out_shape=jax.Sha...  27.6 us

profile of v2, /device:TPU:113, one launch (start us, length us, event | category | flops | bytes accessed | tf_op | source)
XLA Modules:
  0.0 189.0 jit_solution(3864769394591374110)
XLA Ops:
  0.0 56.5 %make_queries.1 = (bf16[16,2,4,64,512]{4,3,2,1,0:T(8,128)(2,1)}, bf16[16,2,4,32,128]{4,3,2,1,0:T(8,128)(2,1)}) custom-call(bf16[16,4,7168]{2,1,0:T(4,128)(2,1)} %hid_ref.1, bf16[7168,8,2,128]{3,2,1,0:T(2,128)(2,1)} %bitcast.16, bf16[1024,7168]{1,0:T(8,128)(2,1)} %bitcast.18, bf16[16,128,512]{2,1,0:T(8,128)(2,1)} %wk_ref.1), custom_call_target="tpu_custom_call" | custom-call | tf_op jit(solution)/shard_map/make_queries/pallas_call | solution.py:195
  56.5 95.7 %attend_merge.1 = bf16[16,64,512]{2,1,0:T(8,128)(2,1)} custom-call(s32[16]{0:T(128)} %lens_ref.1, bf16[16,2,256,512]{3,2,1,0:T(8,128)(2,1)} %bitcast.19, bf16[16,2,128,128]{3,2,1,0:T(8,128)(2,1)} %bitcast.22, bf16[16,2048,512]{2,1,0:T(8,128)(2,1)} %ckv_ref.1, bf16[16,64,2048]{2,1,0:T(8,128)(2,1)} %bitcast.20), custom_call_target="tpu_custom_call" | custom-call | tf_op jit(solution)/shard_map/attend_merge/pallas_call | solution.py:384
  152.3 1.3 reshape.34
  153.6 2.4 %fusion = bf16[16,4,8,2,128]{4,0,1,3,2:T(8,128)(2,1)S(1)} fusion(bf16[8,2,512,128,1]{3,2,4,1,0:T(8,128)(2,1)} %bitcast.21, bf16[16,2,8,4,512]{4,3,2,1,0:T(4,128)(2,1)S(1)} %reshape.34), kind=kOutput, calls=%fused_computation.1 | convolution fusion | flops 134348800 | bytes 3407872 | tf_op jit(solution)/shard_map/bpuqc,upcv->bqupv/dot_general | solution.py:515
  156.0 0.3 copy.11
  156.3 0.9 reshape.36.ov_ref
  157.2 0.9 constant_dynamic-slice_fusion
  158.1 0.7 reshape.37.hid_ref
  158.8 27.6 %project_output.1 = bf16[64,7168]{1,0:T(8,128)(2,1)} custom-call(bf16[64,2048]{1,0:T(8,128)(2,1)} %reshape.36.ov_ref, bf16[64,896]{1,0:T(8,128)(2,1)} %reshape.37.hid_ref, bf16[2048,7168]{1,0:T(8,128)(2,1)} %bitcast.17), custom_call_target="tpu_custom_call" | custom-call | tf_op jit(solution)/shard_map/project_output/pallas_call | solution.py:484
  186.5 2.5 %reshape.39 = bf16[16,4,7168]{2,1,0:T(4,128)(2,1)} reshape(bf16[64,7168]{1,0:T(8,128)(2,1)} %project_output.1) | data formatting | bytes 1835008 | tf_op jit(solution)/shard_map/reshape | solution.py:521

commit v3 on v2

--- a/solution.py
+++ b/solution.py
@@ -10,8 +10,9 @@
 MASK_FILL = -1e30
 LOG2E = 1.4426950408889634
 MESH = pl.DeviceIdType.MESH
-LAG_B, LAG_C, LAG_D = 2, 4, 7
+LAG_B, LAG_C, LAG_D = 1, 3, 6
 CUTS = 4
+AHEAD = 3
 
 
 def remote(src, dst, send_sem, recv_sem, dev):
@@ -50,7 +51,7 @@
     xo = lax.rem(x + 2, chips)
     rows, toks, dim = hid_ref.shape
     pairs, nope = wq_ref.shape[1], wq_ref.shape[3]
-    per_ch = pairs // 2
+    parts = pairs // 2
     depth = dim // CUTS
     f32, bf16 = jnp.float32, jnp.bfloat16
 
@@ -62,13 +63,12 @@
         return pltpu.make_async_copy(wq_ref.at[pl.ds(k * depth, depth), u], wq_buf.at[u, pl.ds(k * depth, depth)],
                                      wq_sem.at[u, k])
 
-    def load_rope(k):
-        n = wr_ref.shape[0] // CUTS
-        return pltpu.make_async_copy(wr_ref.at[pl.ds(k * n, n)], wr_buf.at[pl.ds(k * n, n)], wr_sem.at[k])
+    def load_rope(half, j):
+        return pltpu.make_async_copy(wr_ref.at[half * pairs + j], wr_buf.at[j, half], wr_sem.at[half, j])
 
     load_up = pltpu.make_async_copy(wk_ref, wk_buf, wk_sem)
     for k in range(CUTS):
-        for u in range(per_ch):
+        for u in range(2):
             load(u, k).start()
     load_up.start()
 
@@ -85,9 +85,9 @@
             for side in range(2):
                 wide[k, pl.ds(side * n, n), pl.ds(t * 256, 256)] = res[t * n:(t + 1) * n, side * 256:side * 256 + 256]
 
-    where = lambda p: pl.ds((p % 2) * 2 * 16 + (p // 2) * 16, 16) if p < 4 else pl.ds((p - 4) * 16, 16)
-    own_ref = lambda p: (lat_own if p < 4 else rope_own).at[:, where(p)]
-    all_ref = lambda p, core, block: (lat_all if p < 4 else rope_all).at[:, core, block, where(p)]
+    where = lambda p: pl.ds((p % parts) * 16, 16)
+    own_ref = lambda p: (lat_own if p < parts else rope_own).at[:, where(p)]
+    all_ref = lambda p, core, block: (lat_all if p < parts else rope_all).at[:, core, block, where(p)]
 
     def own(p, kind, dev):
         return remote(own_ref(p), all_ref(p, c, x), send.at[p, kind], recv.at[p, kind], dev)
@@ -103,71 +103,66 @@
 
     def send_own(p):
         own(p, 0, right).start()
-        own(p + 1, 0, right).start()
-        own(p + 1, 1, left).start()
         own(p, 1, left).start()
-        for q in (p, p + 1):
-            own(q, 2, partner).start()
-            keep(q).start()
+        own(p, 2, partner).start()
+        keep(p).start()
 
     def relay(p):
         landed(p, 0, xl, c).wait_recv()
-        pass_on(p, 3, xl, right).start()
+        if p % 2 == 0:
+            pass_on(p, 3, xl, right).start()
         pass_on(p, 4, xl, partner).start()
-        landed(p + 1, 1, xr, c).wait_recv()
-        pass_on(p + 1, 3, xr, left).start()
-        pass_on(p + 1, 5, xr, partner).start()
-        landed(p + 1, 0, xl, c).wait_recv()
-        pass_on(p + 1, 4, xl, partner).start()
         landed(p, 1, xr, c).wait_recv()
+        if p % 2 == 1:
+            pass_on(p, 3, xr, left).start()
         pass_on(p, 5, xr, partner).start()
 
-    for ch in range(2):
-        base = ch * per_ch
+    for q in range(parts):
         acc[...] = jnp.zeros_like(acc)
 
         @pl.loop(0, CUTS)
         def _(k):
-            for u in range(base, base + per_ch):
+            for u in (2 * q, 2 * q + 1):
                 load(u, k).wait()
-            if ch == 0:
-                for u in range(per_ch, pairs):
+            if q < parts - 1:
+                for u in (2 * q + 2, 2 * q + 3):
                     load(u, k).start()
-            else:
-                load_rope(k).start()
-            for j in range(per_ch // 2):
-                w = [wq_buf[base + 2 * j + h, pl.ds(k * depth, depth)].reshape(2 * depth, nope) for h in range(2)]
-                acc[j] += jnp.dot(wide[k], jnp.concatenate(w, axis=1), preferred_element_type=f32)
-
-        if ch == 0:
+            if q == parts - 1:
+                for half in range(2):
+                    load_rope(half, 2 * k).start()
+                    load_rope(half, 2 * k + 1).start()
+            w = [wq_buf[u, pl.ds(k * depth, depth)].reshape(2 * depth, nope) for u in (2 * q, 2 * q + 1)]
+            acc[...] += jnp.dot(wide[k], jnp.concatenate(w, axis=1), preferred_element_type=f32)
+
+        if q == 0:
             load_up.wait()
-        for side in range(2):
-            q_lat = []
-            for u in range(per_ch):
-                q_n = acc[u // 2, pl.ds(side * n, n), pl.ds((u % 2) * nope, nope)].astype(bf16)
-                q_lat.append(jnp.dot(q_n, wk_buf[2 * (base + u) + side], preferred_element_type=f32))
-            pack(q_lat, lat_own, side * 32 + ch * 16)
-        if ch == 0:
+        q_lat = []
+        for h in range(4):
+            q_n = acc[pl.ds((h % 2) * n, n), pl.ds((h // 2) * nope, nope)].astype(bf16)
+            q_lat.append(jnp.dot(q_n, wk_buf[4 * q + h], preferred_element_type=f32))
+        pack(q_lat, lat_own, q * 16)
+        if q == 0:
             pl.semaphore_wait(barrier, 3)
-        send_own(2 * ch)
-    relay(0)
+        send_own(q)
 
     tokens = jnp.concatenate([hid_ref[:, :, t * 128:(t + 1) * 128].reshape(n, 128) for t in range(dim // 128)], axis=1)
-    part = wr_buf.shape[0] // CUTS
-    q_rope = []
-    for k in range(CUTS):
-        load_rope(k).wait()
-        r = lax.dot_general(tokens, wr_buf[pl.ds(k * part, part)], (((1,), (1,)), ((), ())), preferred_element_type=f32)
-        q_rope += [r[:, j * 128:(j + 1) * 128] for j in range(part // 128)]
-    for h in range(2):
-        pack(q_rope[4 * h:4 * h + 4], rope_own, 16 * h)
-    send_own(4)
-    relay(2)
-    relay(4)
-    for p in range(6):
+    for q in range(2):
+        q_rope = []
+        for m in (2 * q, 2 * q + 1):
+            for half in range(2):
+                load_rope(half, 2 * m).wait()
+                load_rope(half, 2 * m + 1).wait()
+            w = wr_buf[pl.ds(2 * m, 2)].reshape(256, dim)
+            r = lax.dot_general(tokens, w, (((1,), (1,)), ((), ())), preferred_element_type=f32)
+            q_rope += [r[:, 0:128], r[:, 128:256]]
+        pack(q_rope, rope_own, 16 * q)
+        send_own(parts + q)
+    for p in range(parts + 2):
+        relay(p)
+    for p in range(parts + 2):
         landed(p, 3, xo, c).wait_recv()
         pass_on(p, 6, xo, partner).start()
-    for p in range(6):
+    for p in range(parts + 2):
         for kind, block in ((2, x), (4, xl), (5, xr), (6, xo)):
             landed(p, kind, block, 1 - c).wait_recv()
         own(p, 0, right).wait_send()
@@ -189,7 +184,7 @@
     gq = heads * toks
     bf16 = jnp.bfloat16
     wq = w_uq.reshape(dim, heads // 2, 2, nope)
-    wr = jnp.transpose(w_qr, (1, 2, 0)).reshape(-1, dim)
+    wr = jnp.transpose(w_qr, (1, 2, 0))
     hbm = pl.BlockSpec(memory_space=pl.ANY)
     dma = pltpu.SemaphoreType.DMA
     return pl.pallas_call(
@@ -199,11 +194,12 @@
         in_specs=[pl.BlockSpec(memory_space=pltpu.VMEM), hbm, hbm, hbm],
         out_specs=[hbm] * 2,
         scratch_shapes=[
-            pltpu.VMEM((heads // 2, dim, 2, nope), bf16), pltpu.VMEM(wr.shape, bf16), pltpu.VMEM(w_uk.shape, bf16),
+            pltpu.VMEM((heads // 2, dim, 2, nope), bf16), pltpu.VMEM((heads // 2, 2) + wr.shape[1:], bf16), pltpu.VMEM(w_uk.shape, bf16),
             pltpu.VMEM((CUTS, 2 * rows * toks, 2 * dim // CUTS), bf16),
-            pltpu.VMEM((heads // 8, 2 * rows * toks, 2 * nope), jnp.float32),
+            pltpu.VMEM((2 * rows * toks, 2 * nope), jnp.float32),
             pltpu.VMEM((rows, gq, width), bf16), pltpu.VMEM((rows, gq // 2, 128), bf16),
-            dma((heads // 2, CUTS)), dma((CUTS,)), dma(()), dma((6, 7)), dma((6, 7)), dma((6,))],
+            dma((heads // 2, CUTS)), dma((2, heads // 2)), dma(()), dma((heads // 4 + 2, 7)),
+            dma((heads // 4 + 2, 7)), dma((heads // 4 + 2,))],
         compiler_params=pltpu.CompilerParams(collective_id=0, has_side_effects=True, vmem_limit_bytes=67_000_000),
         name="make_queries",
     )(hidden, wq, wr, w_uk)
@@ -214,12 +210,12 @@
 
 
 def expand(ml):
-    col = jnp.transpose(jnp.broadcast_to(ml[0:1, :], (128, 128)))
+    col = jnp.transpose(jnp.broadcast_to(ml, (128, 128)))
     return col[0:64, :], col[64:128, :]
 
 
 def compact(m, l):
-    return jnp.transpose(jnp.concatenate([m, l], axis=0))[0:8, :]
+    return jnp.transpose(jnp.concatenate([m, l], axis=0))[0:1, :]
 
 
 def attend_kernel(chips, rows, scale, lens_ref, lat_ref, rope_ref, ckv_ref, kr_ref, out_ref,
@@ -308,8 +304,6 @@
             o = home_o[r, x, :, at] * fa + two_o[r, 0, :, at] * fb + two_o[r, 1, :, at] * fc
             out_ref[0, :, at] = (o / l).astype(out_ref.dtype)
 
-    on_row(LAG_B, lambda cp: cp.wait_recv(), range(0, 2))
-    on_row(LAG_C, lambda cp: cp.wait_recv(), range(2, 6))
     on_row(LAG_D, lambda cp: cp.wait_recv(), range(6, 10))
 
     @pl.when(i < rows)
@@ -347,11 +341,13 @@
                 o_ref[i, g] = o[at]
                 ml_ref[i, g] = compact(m[at], l[at])
 
+        finish()
+        scores(0, 1 - c)
+        scores(1, c)
+        on_row(LAG_B, lambda cp: cp.wait_recv(), range(0, 2))
+        on_row(LAG_C, lambda cp: cp.wait_recv(), range(2, 6))
         merge_pair()
-        scores(0, 1 - c)
         merge_half()
-        scores(1, c)
-        finish()
         ml0 = weigh(0)
         mix(0, *ml0, away_o, away_ml)
         ml1 = weigh(1)
@@ -359,6 +355,8 @@
 
     @pl.when(i >= rows)
     def _():
+        on_row(LAG_B, lambda cp: cp.wait_recv(), range(0, 2))
+        on_row(LAG_C, lambda cp: cp.wait_recv(), range(2, 6))
         merge_pair()
         merge_half()
         finish()
@@ -393,11 +391,11 @@
         out_specs=pl.BlockSpec((1, gq, width), lambda i: (jnp.maximum(i - LAG_D, 0), 0, 0)),
         scratch_shapes=[
             pltpu.VMEM((2, nq, local_len), f32), pltpu.VMEM((2, nq, local_len), bf16),
-            pltpu.VMEM((rows + 1, chips, gq, width), f32), pltpu.VMEM((rows + 1, chips, 8, 128), f32),
-            pltpu.VMEM((rows + 1, chips, gq, width), f32), pltpu.VMEM((rows + 1, chips, 8, 128), f32),
-            pltpu.VMEM((rows + 1, chips, gq, width), f32), pltpu.VMEM((rows + 1, chips, 8, 128), f32),
-            pltpu.VMEM((rows + 1, 2, gq // 2, width), f32), pltpu.VMEM((rows + 1, 2, 8, 128), f32),
-            pltpu.VMEM((rows + 1, 2, gq, width), f32), pltpu.VMEM((rows + 1, 2, 8, 128), f32),
+            pltpu.VMEM((rows + 1, chips, gq, width), f32), pltpu.VMEM((rows + 1, chips, 1, 128), f32),
+            pltpu.VMEM((rows + 1, chips, gq, width), f32), pltpu.VMEM((rows + 1, chips, 1, 128), f32),
+            pltpu.VMEM((rows + 1, chips, gq, width), f32), pltpu.VMEM((rows + 1, chips, 1, 128), f32),
+            pltpu.VMEM((rows + 1, 2, gq // 2, width), f32), pltpu.VMEM((rows + 1, 2, 1, 128), f32),
+            pltpu.VMEM((rows + 1, 2, gq, width), f32), pltpu.VMEM((rows + 1, 2, 1, 128), f32),
             pltpu.SemaphoreType.DMA((rows, 10)), pltpu.SemaphoreType.DMA((rows, 10))],
         compiler_params=pltpu.CompilerParams(collective_id=1, has_side_effects=True,
                                              dimension_semantics=("arbitrary",), vmem_limit_bytes=67_000_000),
@@ -405,96 +403,148 @@
     )(lens, lat, rope, ckv, kr)
 
 
-def output_kernel(chips, ov_ref, hid_ref, w_ref, out_ref, w_buf, away, near, home, far,
-                  w_sem, send, recv):
+def unpack(ref, slot):
+    rows = ref.shape[0]
+    tiles = [ref[b, pl.ds(slot, 16)].astype(jnp.float32) for b in range(rows)]
+    vals = []
+    for h in range(2):
+        even = jnp.concatenate([t[8 * h:8 * h + 8] for t in tiles[0::2]], axis=0)
+        odd = jnp.concatenate([t[8 * h:8 * h + 8] for t in tiles[1::2]], axis=0)
+        n = even.shape[0]
+        low = lax.rem(lax.broadcasted_iota(jnp.int32, even.shape, 0), 8) < 4
+        vals += [jnp.where(low, even, pltpu.roll(odd, 4, 0)), jnp.where(low, pltpu.roll(even, n - 4, 0), odd)]
+    return [v.astype(ref.dtype) for v in vals]
+
+
+def output_kernel(chips, o_ref, hid_ref, wv_ref, w_ref, out_ref, o_buf, hid_buf, wv_buf, ov, w_buf,
+                  away, near, home, one, two, in_sem, w_sem, send, recv):
     x, c, xr, xl, right, left, partner = place(chips)
-    me = 2 * x + c
     xo = lax.rem(x + 2, chips)
     cols = w_buf.shape[2]
+    rows, toks = out_ref.shape[:2]
     span = lambda dev: pl.ds(pl.multiple_of(dev * cols, 128), cols)
     dests = (xo, xr, xl, x)
-
-    def load(k, first):
-        core = 1 - c if first else c
-        n = 2 * k + (0 if first else 1)
-        return pltpu.make_async_copy(w_ref.at[:, span(2 * dests[k] + core)], w_buf.at[n], w_sem.at[n])
-
+    order = []
     for k in range(chips):
-        load(k, True).start()
-        load(k, False).start()
-    peers = tuple(2 * d + c for d in dests[:3])
-    greet(peers + (partner,))
+        order += [2 * dests[k] + 1 - c, 2 * dests[k] + c]
+
+    def load(n):
+        return pltpu.make_async_copy(w_ref.at[:, span(order[n])], w_buf.at[n], w_sem.at[n])
+
+    firsts = [pltpu.make_async_copy(o_ref, o_buf, in_sem.at[0]), pltpu.make_async_copy(wv_ref, wv_buf, in_sem.at[1]),
+              pltpu.make_async_copy(hid_ref.at[:, :, span(2 * x + c)], hid_buf, in_sem.at[2])]
+    for cp in firsts:
+        cp.start()
+    for n in range(AHEAD):
+        load(n).start()
+    greet((right, left, partner))
+
+    firsts[0].wait()
+    firsts[1].wait()
+    value = wv_buf.shape[2]
+    for q in range(wv_buf.shape[0] // 4):
+        for h, o_lat in enumerate(unpack(o_buf, 16 * q)):
+            ov[:, pl.ds((4 * q + h) * value, value)] = jnp.dot(
+                o_lat, wv_buf[4 * q + h], preferred_element_type=jnp.float32).astype(ov.dtype)
+
+    tokens = ov.shape[0]
+    first, second = pl.ds(0, tokens // 2), pl.ds(tokens // 2, tokens // 2)
+
+    def project(n):
+        load(n).wait()
+        if n + AHEAD < 2 * chips:
+            load(n + AHEAD).start()
+        return jnp.dot(ov[...], w_buf[n], preferred_element_type=jnp.float32)
 
     def swap(k):
         return remote(away.at[k], near.at[k], send.at[0, k], recv.at[0, k], partner)
 
-    def reduce(k):
-        return remote(home.at[k], far.at[k], send.at[1, k], recv.at[1, k], peers[k])
-
+    def hop(kind):
+        src, dst, dev = ((home.at[0, first], one.at[0], right), (home.at[0, second], one.at[1], left),
+                         (home.at[1], two.at[0], right), (home.at[2], two.at[1], left))[kind]
+        return remote(src, dst, send.at[1, kind], recv.at[1, kind], dev)
+
+    away[0] = project(0)
+    swap(0).start()
     for k in range(chips):
-        load(k, True).wait()
-        away[k] = jnp.dot(ov_ref[...], w_buf[2 * k], preferred_element_type=jnp.float32)
-        swap(k).start()
-        load(k, False).wait()
-        home[k] = jnp.dot(ov_ref[...], w_buf[2 * k + 1], preferred_element_type=jnp.float32)
+        home[k] = project(2 * k + 1)
+        if k + 1 < chips:
+            away[k + 1] = project(2 * k + 2)
+            swap(k + 1).start()
         swap(k).wait_recv()
         home[k] = home[k] + near[k]
-        if k < chips - 1:
-            reduce(k).start()
-    for k in range(chips - 1):
-        reduce(k).wait_recv()
-    y = home[chips - 1] + far[0] + far[1] + far[2]
-    out_ref[:, span(me)] = (hid_ref[...].astype(jnp.float32) + y).astype(out_ref.dtype)
-
-    def spread(k):
-        return remote(out_ref.at[:, span(me)], out_ref.at[:, span(me)], send.at[2, k], recv.at[2, k], peers[k])
-
-    def mirror(k):
-        ref = out_ref.at[:, span(2 * dests[k] + c)]
-        return remote(ref, ref, send.at[3, k], recv.at[3, k], partner)
-
-    def landed(kind, k, dev):
-        ref = out_ref.at[:, span(dev)]
-        return remote(ref, ref, send.at[kind, k], recv.at[kind, k], partner)
-
-    for k in range(chips - 1):
-        spread(k).start()
-    mirror(3).start()
-    source = (xo, xl, xr)
-    slot = (0, 2, 1)
-    for k in (1, 2, 0):
-        landed(2, k, 2 * source[k] + c).wait_recv()
-        mirror(slot[k]).start()
-    for k in range(chips):
-        landed(3, k, 2 * ((xo, xr, xl, x)[k]) + 1 - c).wait_recv()
+        if k == 0:
+            hop(0).start()
+            hop(1).start()
+        if k == 1:
+            hop(0).wait_recv()
+            home[1, first] = home[1, first] + one[0]
+            hop(2).start()
+        if k == 2:
+            hop(1).wait_recv()
+            home[2, second] = home[2, second] + one[1]
+            hop(3).start()
+    firsts[2].wait()
+    hop(2).wait_recv()
+    hop(3).wait_recv()
+    y = home[chips - 1] + two[0] + two[1]
+    out_ref[:, :, span(2 * x + c)] = (hid_buf[...].astype(jnp.float32) + y.reshape(rows, toks, cols)).astype(out_ref.dtype)
+
+    whole, top, low = pl.ds(0, rows), pl.ds(0, rows // 2), pl.ds(rows // 2, rows // 2)
+
+    def give(kind, part, block, core, dev):
+        ref = out_ref.at[part, :, span(2 * block + core)]
+        return remote(ref, ref, send.at[2, kind], recv.at[2, kind], dev)
+
+    sends = [give(0, whole, x, c, right), give(1, whole, x, c, left), give(2, whole, x, c, partner),
+             give(3, top, xl, c, right), give(4, low, xr, c, left),
+             give(5, whole, xl, c, partner), give(6, whole, xr, c, partner),
+             give(7, top, xo, c, partner), give(8, low, xo, c, partner)]
+    for n in (0, 1, 2):
+        sends[n].start()
+    give(0, whole, xl, c, partner).wait_recv()
+    sends[3].start()
+    sends[5].start()
+    give(1, whole, xr, c, partner).wait_recv()
+    sends[4].start()
+    sends[6].start()
+    give(3, top, xo, c, partner).wait_recv()
+    sends[7].start()
+    give(4, low, xo, c, partner).wait_recv()
+    sends[8].start()
+    for kind, part, block in ((2, whole, x), (5, whole, xl), (6, whole, xr), (7, top, xo), (8, low, xo)):
+        give(kind, part, block, 1 - c, partner).wait_recv()
     for k in range(chips):
         swap(k).wait_send()
-        mirror(k).wait_send()
-        if k < chips - 1:
-            reduce(k).wait_send()
-            spread(k).wait_send()
-
-
-def output(chips, o_val, hidden, w_o):
-    tokens, depth = o_val.shape
-    dim = w_o.shape[1]
+        hop(k).wait_send()
+    for cp in sends:
+        cp.wait_send()
+
+
+def output(chips, o_lat, hidden, w_uv, w_o):
+    rows, toks, dim = hidden.shape
+    tokens = rows * toks
+    depth = w_o.shape[0]
     cols = dim // (2 * chips)
     f32 = jnp.float32
-    vmem = pl.BlockSpec(memory_space=pltpu.VMEM)
+    vmem, hbm = pl.BlockSpec(memory_space=pltpu.VMEM), pl.BlockSpec(memory_space=pl.ANY)
+    dma = pltpu.SemaphoreType.DMA
     return pl.pallas_call(
         functools.partial(output_kernel, chips),
-        out_shape=jax.ShapeDtypeStruct((tokens, dim), hidden.dtype),
-        in_specs=[vmem, vmem, pl.BlockSpec(memory_space=pl.ANY)],
+        out_shape=jax.ShapeDtypeStruct(hidden.shape, hidden.dtype),
+        in_specs=[hbm] * 4,
         out_specs=vmem,
         scratch_shapes=[
+            pltpu.VMEM(o_lat.shape, o_lat.dtype), pltpu.VMEM((rows, toks, cols), hidden.dtype),
+            pltpu.VMEM(w_uv.shape, w_uv.dtype), pltpu.VMEM((tokens, depth), o_lat.dtype),
             pltpu.VMEM((2 * chips, depth, cols), w_o.dtype),
             pltpu.VMEM((chips, tokens, cols), f32), pltpu.VMEM((chips, tokens, cols), f32),
-            pltpu.VMEM((chips, tokens, cols), f32), pltpu.VMEM((chips - 1, tokens, cols), f32),
-            pltpu.SemaphoreType.DMA((2 * chips,)),
-            pltpu.SemaphoreType.DMA((4, chips)), pltpu.SemaphoreType.DMA((4, chips))],
+            pltpu.VMEM((chips, tokens, cols), f32), pltpu.VMEM((2, tokens // 2, cols), f32),
+            pltpu.VMEM((2, tokens, cols), f32),
+            dma((3,)), dma((2 * chips,)), dma((3, 9)), dma((3, 9))],
         compiler_params=pltpu.CompilerParams(collective_id=2, has_side_effects=True, vmem_limit_bytes=60_000_000),
         name="project_output",
-    )(o_val, hidden, w_o)
+    )(o_lat, hidden, w_uv, w_o)
 
 
 def solution(mesh):
@@ -506,19 +556,12 @@
         rope_dim = w_qr.shape[2]
         value = w_uv.shape[2]
         score_scale = (nope + rope_dim) ** -0.5
-        f32, bf16 = jnp.float32, jnp.bfloat16
         gq = toks * heads
         lat_all, rope_all = queries(chips, hidden, w_uq, w_qr, w_uk)
         o_lat = attend(chips, score_scale, cache_lens,
                        lat_all.reshape(rows, 2, chips * gq, width),
                        rope_all.reshape(rows, 2, chips * gq // 2, 2 * rope_dim), c_kv, jnp.swapaxes(k_r, 1, 2))
-        o_val = jnp.einsum("bpuqc,upcv->bqupv", o_lat.reshape(rows, 2, heads // 2, toks, width),
-                           w_uv.reshape(heads // 2, 2, width, value), preferred_element_type=f32).astype(bf16)
-        cols = dim // (2 * chips)
-        own = lax.dynamic_slice_in_dim(hidden, lax.axis_index("seq") * cols, cols, axis=2)
-        out = output(chips, o_val.reshape(rows * toks, heads * value), own.reshape(rows * toks, cols),
-                     w_o.reshape(heads * value, dim))
-        return out.reshape(rows, toks, dim)
+        return output(chips, o_lat, hidden, w_uv, w_o.reshape(heads * value, dim))
 
     specs_in = (P("batch", None, None), P("batch"), P("batch", "seq", None), P("batch", "seq", None),
                 P(None, "seq", None), P(None, "seq", None), P("seq", None, None), P("seq", None, None),

time: 189 us -> 174 us (0.921)
  Pallas kernels: 180 us -> 172 us
  local copies, waits for them, and re-layouts: 6.65 us -> 2.42 us
  matrix products: 2.39 us -> 0 us
    reshape x4 -> x0, local copies, waits for them, and re-layouts: 5.44 us -> none  [the longest x1 2.52 us: local_step(): return out.reshape(rows, toks, dim)]
    pallas_call x1, Pallas kernels: 95.7 us -> 91 us  [attend(): pl.pallas_call(functools.partial(attend_kernel, chips, rows, scale), grid...]
    pallas_call x1, Pallas kernels: 56.5 us -> 52.4 us  [queries(): pl.pallas_call(functools.partial(query_kernel, chips), out_shape=[jax.Sha...]
    unnamed x0 -> x1, local copies, waits for them, and re-layouts: none -> 2.42 us
    dot_general x1 -> x0, matrix products: 2.39 us -> none  [local_step(): jnp.einsum('bpuqc,upcv->bqupv', o_lat.reshape(rows, 2, heads // 2, toks,...]
where the time goes in v3:
time: 174 us
  Pallas kernels  172 us (99%)
  local copies, waits for them, and re-layouts  2.42 us (1%)
    pallas_call x1, Pallas kernels, attend(): pl.pallas_call(functools.partial(attend_kernel, chips, rows, scale), grid...  91 us
    pallas_call x1, Pallas kernels, queries(): pl.pallas_call(functools.partial(query_kernel, chips), out_shape=[jax.Sha...  52.4 us
    pallas_call x1, Pallas kernels, output(): pl.pallas_call(functools.partial(output_kernel, chips), out_shape=jax.Sha...  28.4 us

profile of v3, /device:TPU:113, one launch (start us, length us, event | category | flops | bytes accessed | tf_op | source)
XLA Modules:
  0.0 174.2 jit_solution(8927887532989293737)
XLA Ops:
  0.0 52.4 %make_queries.1 = (bf16[16,2,4,64,512]{4,3,2,1,0:T(8,128)(2,1)}, bf16[16,2,4,32,128]{4,3,2,1,0:T(8,128)(2,1)}) custom-call(bf16[16,4,7168]{2,1,0:T(4,128)(2,1)} %hid_ref.3, bf16[7168,8,2,128]{3,2,1,0:T(2,128)(2,1)} %bitcast.6, bf16[16,64,7168]{2,1,0:T(8,128)(2,1)} %bitcast.8, bf16[16,128,512]{2,1,0:T(8,128)(2,1)} %wk_ref.1), custom_call_target="tpu_custom_call" | custom-call | tf_op jit(solution)/shard_map/make_queries/pallas_call | solution.py:190
  52.4 91.0 %attend_merge.1.o_ref = bf16[16,64,512]{2,1,0:T(8,128)(2,1)} custom-call(s32[16]{0:T(128)} %lens_ref.1, bf16[16,2,256,512]{3,2,1,0:T(8,128)(2,1)} %bitcast.9, bf16[16,2,128,128]{3,2,1,0:T(8,128)(2,1)} %bitcast.11, bf16[16,2048,512]{2,1,0:T(8,128)(2,1)} %ckv_ref.1, bf16[16,64,2048]{2,1,0:T(8,128)(2,1)} %bitcast.10), custom_call_target="tpu_custom_call" | custom-call | tf_op jit(solution)/shard_map/attend_merge/pallas_call | solution.py:382
  143.4 28.4 %project_output.1 = bf16[16,4,7168]{2,1,0:T(4,128)(2,1)} custom-call(bf16[16,64,512]{2,1,0:T(8,128)(2,1)} %attend_merge.1.o_ref, bf16[16,4,7168]{2,1,0:T(4,128)(2,1)} %hid_ref.3, bf16[16,512,128]{2,1,0:T(8,128)(2,1)} %wv_ref.1, bf16[2048,7168]{1,0:T(8,128)(2,1)} %bitcast.7), custom_call_target="tpu_custom_call" | custom-call | tf_op jit(solution)/shard_map/project_output/pallas_call | solution.py:532
  171.8 2.4 %copy.11 = bf16[16,4,7168]{2,1,0:T(4,128)(2,1)} copy(bf16[16,4,7168]{2,1,0:T(4,128)(2,1)} %project_output.1) | data formatting | bytes 1835008

commit v4 on v3

v4 whole, which is shorter than its diff:
```python
import functools

import jax
import jax.numpy as jnp
from jax import lax
from jax.experimental import pallas as pl
from jax.experimental.pallas import tpu as pltpu
from jax.sharding import PartitionSpec as P

MASK_FILL = -1e30
LOG2E = 1.4426950408889634
MESH = pl.DeviceIdType.MESH
LAG_B, LAG_C, LAG_D = 1, 3, 6
CUTS = 4
AHEAD = 3
AWAY, HOME, PAIR, ONE, TWO = 4, 10, 4, 6, 8


def remote(src, dst, send_sem, recv_sem, dev):
    return pltpu.make_async_remote_copy(src_ref=src, dst_ref=dst, send_sem=send_sem, recv_sem=recv_sem,
                                        device_id={"seq": dev}, device_id_type=MESH)


def place(chips):
    me = lax.axis_index("seq")
    x, c = me // 2, lax.rem(me, 2)
    xr, xl = lax.rem(x + 1, chips), lax.rem(x + chips - 1, chips)
    return x, c, xr, xl, 2 * xr + c, 2 * xl + c, 2 * x + 1 - c


def greet(devs):
    barrier = pltpu.get_barrier_semaphore()
    for dev in devs:
        pl.semaphore_signal(barrier, inc=1, device_id={"seq": dev}, device_id_type=MESH)
    pl.semaphore_wait(barrier, len(devs))


def pack(vals, dst, slot):
    n = vals[0].shape[0]
    low = lax.rem(lax.broadcasted_iota(jnp.int32, vals[0].shape, 0), 8) < 4
    even = [jnp.where(low, p, pltpu.roll(q, 4, 0)) for p, q in (vals[:2], vals[2:])]
    odd = [jnp.where(low, pltpu.roll(p, n - 4, 0), q) for p, q in (vals[:2], vals[2:])]
    for v in range(n // 8):
        at = slice(8 * v, 8 * v + 8)
        for side, both in ((0, even), (1, odd)):
            dst[2 * v + side, pl.ds(slot, 16)] = jnp.concatenate([both[0][at], both[1][at]], axis=0).astype(dst.dtype)


def token(row):
    return lax.rem(row, 4)


def expand(ml):
    col = jnp.transpose(jnp.broadcast_to(ml, (128, 128)))
    return col[0:64, :], col[64:128, :]


def compact(m, l):
    return jnp.transpose(jnp.concatenate([m, l], axis=0))[0:1, :]


def attend_kernel(chips, rows, scale, lens_ref, hid_ref, wq_ref, wr_ref, wk_ref, ckv_ref, kr_ref, out_ref,
                  wq_buf, wr_buf, wk_buf, wide, acc, lat_all, rope_all, s_buf, p_buf,
                  away_o, away_ml, home_o, home_ml, d2d_o, d2d_ml, one_o, one_ml, two_o, two_ml,
                  wq_sem, wr_sem, wk_sem, q_send, q_recv, send, recv):
    x, c, xr, xl, right, left, partner = place(chips)
    xo = lax.rem(x + 2, chips)
    i = pl.program_id(0)
    f32, bf16 = jnp.float32, jnp.bfloat16
    toks, dim = hid_ref.shape[1:]
    n = rows * toks
    pairs, nope = wq_ref.shape[1], wq_ref.shape[3]
    quarters = pairs // 2
    depth = dim // CUTS
    local_len, width = ckv_ref.shape[1:]
    gq = lat_all.shape[3]
    nq = chips * gq
    hq = gq // 2
    k2 = scale * LOG2E
    lanes = [pl.ds(j * 128, 128) for j in range(width // 128)]

    top, low, every = pl.ds(0, rows // 2), pl.ds(rows // 2, rows // 2), pl.ds(0, rows)
    pieces = [(lat_all, every, pl.ds(0, 16), 0), (lat_all, every, pl.ds(16, 16), 1)]
    for part, turn in ((top, 0), (low, 1)):
        pieces += [(lat_all, part, pl.ds(32, 16), 0), (lat_all, part, pl.ds(48, 16), 1),
                   (rope_all, part, pl.ds(0, hq), turn)]

    def give(p, kind, block, core, dev):
        array, part, queries, _ = pieces[p]
        ref = array.at[part, core, block, queries]
        return remote(ref, ref, q_send.at[p, kind], q_recv.at[p, kind], dev)

    def send_own(p):
        give(p, 0, x, c, right).start()
        give(p, 1, x, c, left).start()
        give(p, 2, x, c, partner).start()

    def second_hop(p):
        return give(p, 3, xr, c, left) if pieces[p][3] else give(p, 3, xl, c, right)

    def relay(p):
        give(p, 0, xl, c, partner).wait_recv()
        if pieces[p][3] == 0:
            second_hop(p).start()
        give(p, 4, xl, c, partner).start()
        give(p, 1, xr, c, partner).wait_recv()
        if pieces[p][3] == 1:
            second_hop(p).start()
        give(p, 5, xr, c, partner).start()

    def relay_far(p):
        give(p, 3, xo, c, partner).wait_recv()
        give(p, 6, xo, c, partner).start()

    def complete(p):
        for kind, block in ((2, x), (4, xl), (5, xr), (6, xo)):
            give(p, kind, block, 1 - c, partner).wait_recv()

    def sent(p):
        give(p, 0, x, c, right).wait_send()
        give(p, 1, x, c, left).wait_send()
        give(p, 2, x, c, partner).wait_send()
        second_hop(p).wait_send()
        give(p, 4, xl, c, partner).wait_send()
        give(p, 5, xr, c, partner).wait_send()
        give(p, 6, xo, c, partner).wait_send()

    def make_queries():
        barrier = pltpu.get_barrier_semaphore()
        for dev in (right, left, partner):
            pl.semaphore_signal(barrier, inc=1, device_id={"seq": dev}, device_id_type=MESH)

        def load(q, h, k):
            at = pl.ds(k * depth, depth)
            return pltpu.make_async_copy(wq_ref.at[at, 2 * q + h], wq_buf.at[h, at], wq_sem.at[q, h, k])

        def load_rope(half, j):
            return pltpu.make_async_copy(wr_ref.at[half * pairs + j], wr_buf.at[j % 4, half], wr_sem.at[half, j])

        load_up = pltpu.make_async_copy(wk_ref, wk_buf, wk_sem)
        for k in range(CUTS):
            for h in range(2):
                load(0, h, k).start()
        load_up.start()
        for j in range(4):
            for half in range(2):
                load_rope(half, j).start()

        lane = lax.broadcasted_iota(jnp.int32, (128, 512), 1)
        src = lax.broadcasted_iota(jnp.int32, (128, 512), 0)
        spread = jnp.where(lax.rem(lane, 256) == 2 * src + lane // 256, 1.0, 0.0).astype(bf16)
        tiles = depth // 128
        for k in range(CUTS):
            stack = jnp.concatenate([hid_ref[:, :, (k * tiles + t) * 128:(k * tiles + t + 1) * 128].reshape(n, 128)
                                     for t in range(tiles)], axis=0)
            res = jnp.dot(stack, spread, preferred_element_type=f32).astype(bf16)
            for t in range(tiles):
                for side in range(2):
                    wide[k, pl.ds(side * n, n), pl.ds(t * 256, 256)] = res[t * n:(t + 1) * n,
                                                                           side * 256:side * 256 + 256]

        for q in range(quarters):
            acc[...] = jnp.zeros_like(acc)

            @pl.loop(0, CUTS)
            def _(k):
                for h in range(2):
                    load(q, h, k).wait()
                w = [wq_buf[h, pl.ds(k * depth, depth)].reshape(2 * depth, nope) for h in range(2)]
                acc[...] += jnp.dot(wide[k], jnp.concatenate(w, axis=1), preferred_element_type=f32)
                if q < quarters - 1:
                    for h in range(2):
                        load(q + 1, h, k).start()

            if q == 0:
                load_up.wait()
            q_lat = []
            for h in range(4):
                q_n = acc[pl.ds((h % 2) * n, n), pl.ds((h // 2) * nope, nope)].astype(bf16)
                q_lat.append(jnp.dot(q_n, wk_buf[4 * q + h], preferred_element_type=f32))
            pack(q_lat, lat_all.at[:, c, x], q * 16)
            if q == 0:
                pl.semaphore_wait(barrier, 3)
            send_own(q)

        tokens = jnp.concatenate([hid_ref[:, :, t * 128:(t + 1) * 128].reshape(n, 128) for t in range(dim // 128)],
                                 axis=1)
        for q in range(2):
            q_rope = []
            for m in (2 * q, 2 * q + 1):
                for half in range(2):
                    load_rope(half, 2 * m).wait()
                    load_rope(half, 2 * m + 1).wait()
                w = wr_buf[pl.ds(2 * m % 4, 2)].reshape(256, dim)
                r = lax.dot_general(tokens, w, (((1,), (1,)), ((), ())), preferred_element_type=f32)
                if q == 0:
                    for half in range(2):
                        load_rope(half, 2 * m + 4).start()
                        load_rope(half, 2 * m + 5).start()
                q_rope += [r[:, 0:128], r[:, 128:256]]
            pack(q_rope, rope_all.at[:, c, x], 16 * q)
        send_own(4)
        for p in range(5):
            relay(p)
        for p in range(5, 8):
            send_own(p)
        for p in range(5):
            relay_far(p)
        for p in range(5):
            complete(p)

    def moves(r):
        a, h, d, e, t = (lax.rem(r, count) for count in (AWAY, HOME, PAIR, ONE, TWO))
        return (
            (away_o.at[a], d2d_o.at[d], partner),
            (away_ml.at[r], d2d_ml.at[r], partner),
            (home_o.at[h, xo, pl.ds(0, hq)], one_o.at[e, 0], right),
            (home_ml.at[r, xo], one_ml.at[r, 0], right),
            (home_o.at[h, xo, pl.ds(hq, hq)], one_o.at[e, 1], left),
            (home_ml.at[r, xo], one_ml.at[r, 1], left),
            (home_o.at[h, xr], two_o.at[t, 0], right),
            (home_ml.at[r, xr], two_ml.at[r, 0], right),
            (home_o.at[h, xl], two_o.at[t, 1], left),
            (home_ml.at[r, xl], two_ml.at[r, 1], left),
        )

    def copy(r, kind):
        src, dst, dev = moves(r)[kind]
        return remote(src, dst, send.at[r, kind], recv.at[r, kind], dev)

    def late(lag):
        return jnp.where((i >= lag) & (i < rows + lag), i - lag, rows)

    def slot(r, count):
        return jnp.where(r < rows, lax.rem(r, count), count)

    def on_row(lag, act, kinds):
        @pl.when((i >= lag) & (i < rows + lag))
        def _():
            for kind in kinds:
                act(copy(i - lag, kind))

    def merge_pair():
        r = late(LAG_B)
        h, d = slot(r, HOME), slot(r, PAIR)
        for g in range(chips):
            ma, la = expand(home_ml[r, g])
            mb, lb = expand(d2d_ml[r, g])
            m = jnp.maximum(ma, mb)
            fa, fb = jnp.exp2((ma - m) * k2), jnp.exp2((mb - m) * k2)
            for at in lanes:
                home_o[h, g, :, at] = home_o[h, g, :, at] * fa + d2d_o[d, g, :, at] * fb
            home_ml[r, g] = compact(m, la * fa + lb * fb)

    def merge_half():
        r = late(LAG_C)
        h, e = slot(r, HOME), slot(r, ONE)
        for side, g in ((0, xr), (1, xl)):
            part = slice(side * hq, (side + 1) * hq)
            ma, la = expand(home_ml[r, g])
            mb, lb = expand(one_ml[r, side])
            m = jnp.maximum(ma, mb)[part]
            fa, fb = jnp.exp2((ma[part] - m) * k2), jnp.exp2((mb[part] - m) * k2)
            for at in lanes:
                home_o[h, g, pl.ds(side * hq, hq), at] = (home_o[h, g, pl.ds(side * hq, hq), at] * fa
                                                          + one_o[e, side, :, at] * fb)
            l = la[part] * fa + lb[part] * fb
            if side == 0:
                m, l = jnp.concatenate([m, ma[hq:]], axis=0), jnp.concatenate([l, la[hq:]], axis=0)
            else:
                m, l = jnp.concatenate([ma[:hq], m], axis=0), jnp.concatenate([la[:hq], l], axis=0)
            home_ml[r, g] = compact(m, l)

    def finish():
        r = late(LAG_D)
        h, e = slot(r, HOME), slot(r, TWO)
        ma, la = expand(home_ml[r, x])
        mb, lb = expand(two_ml[r, 0])
        mc, lc = expand(two_ml[r, 1])
        m = jnp.maximum(ma, jnp.maximum(mb, mc))
        fa, fb, fc = jnp.exp2((ma - m) * k2), jnp.exp2((mb - m) * k2), jnp.exp2((mc - m) * k2)
        l = la * fa + lb * fb + lc * fc
        for at in lanes:
            o = home_o[h, x, :, at] * fa + two_o[e, 0, :, at] * fb + two_o[e, 1, :, at] * fc
            out_ref[0, :, at] = (o / l).astype(out_ref.dtype)

    @pl.when(i == 0)
    def _():
        make_queries()

    @pl.when(i == rows // 2)
    def _():
        for p in range(5, 8):
            complete(p)

    @pl.when((i >= AWAY) & (i < rows + AWAY))
    def _():
        for kind in range(0, 2):
            copy(i - AWAY, kind).wait_send()

    @pl.when(i >= HOME)
    def _():
        for kind in range(2, 10):
            copy(i - HOME, kind).wait_send()

    on_row(LAG_D, lambda cp: cp.wait_recv(), range(6, 10))

    @pl.when(i < rows)
    def _():
        base = (2 * x + c) * local_len
        row = jnp.minimum(i, rows - 1)
        seen = lens_ref[row] - base
        a, h = lax.rem(row, AWAY), lax.rem(row, HOME)
        col = lax.broadcasted_iota(jnp.int32, (nq, local_len), 1)
        tok = token(lax.broadcasted_iota(jnp.int32, (nq, 1), 0))
        visible = col <= seen + tok
        contract = (((1,), (1,)), ((), ()))

        def scores(k, block):
            lat = lat_all[row, block].reshape(nq, width)
            rope = jnp.concatenate([rope_all[row, block, g][:, e * 64:(e + 1) * 64] for g in range(chips) for e in range(2)],
                                   axis=0)
            s = lax.dot_general(lat, ckv_ref[0], contract, preferred_element_type=f32)
            s = s + jnp.dot(rope, kr_ref[0], preferred_element_type=f32)
            s_buf[k] = jnp.where(visible, s, MASK_FILL)

        def weigh(k):
            s = s_buf[k]
            m = jnp.max(s, axis=1, keepdims=True)
            p = jnp.exp2((s - m) * k2)
            l = jnp.sum(p, axis=1, keepdims=True)
            p_buf[k] = p.astype(bf16)
            return m, l

        def mix(k, m, l, o_ref, to, ml_ref):
            o = jnp.dot(p_buf[k], ckv_ref[0], preferred_element_type=f32)
            m = jnp.broadcast_to(m, (nq, 128))
            l = jnp.broadcast_to(l, (nq, 128))
            for g in range(chips):
                at = slice(g * gq, (g + 1) * gq)
                o_ref[to, g] = o[at]
                ml_ref[row, g] = compact(m[at], l[at])

        finish()
        scores(0, 1 - c)
        scores(1, c)
        on_row(LAG_B, lambda cp: cp.wait_recv(), range(0, 2))
        on_row(LAG_C, lambda cp: cp.wait_recv(), range(2, 6))
        merge_pair()
        merge_half()
        ml0 = weigh(0)
        mix(0, *ml0, away_o, a, away_ml)
        ml1 = weigh(1)
        mix(1, *ml1, home_o, h, home_ml)

    @pl.when(i >= rows)
    def _():
        on_row(LAG_B, lambda cp: cp.wait_recv(), range(0, 2))
        on_row(LAG_C, lambda cp: cp.wait_recv(), range(2, 6))
        merge_pair()
        merge_half()
        finish()

    on_row(0, lambda cp: cp.start(), range(0, 2))
    on_row(LAG_B, lambda cp: cp.start(), range(2, 6))
    on_row(LAG_C, lambda cp: cp.start(), range(6, 10))

    @pl.when(i == 0)
    def _():
        relay(5)

    @pl.when(i == 1)
    def _():
        relay(6)
        relay(7)

    @pl.when(i == 3)
    def _():
        for p in range(5, 8):
            relay_far(p)

    @pl.when(i == rows + LAG_D - 1)
    def _():
        for p in range(8):
            sent(p)

        @pl.loop(rows + LAG_D - HOME, rows)
        def _(r):
            for kind in range(2, 10):
                copy(r, kind).wait_send()


def attend(chips, scale, lens, hidden, w_uq, w_qr, w_uk, ckv, kr):
    rows, toks, dim = hidden.shape
    heads, nope, width = w_uk.shape
    gq = heads * toks
    nq = chips * gq
    local_len = ckv.shape[1]
    wq = w_uq.reshape(dim, heads // 2, 2, nope)
    wr = jnp.transpose(w_qr, (1, 2, 0))
    row = lambda i: jnp.minimum(i, rows - 1)
    f32, bf16 = jnp.float32, jnp.bfloat16
    hbm = pl.BlockSpec(memory_space=pl.ANY)
    dma = pltpu.SemaphoreType.DMA
    return pl.pallas_call(
        functools.partial(attend_kernel, chips, rows, scale),
        grid=(rows + LAG_D,),
        out_shape=jax.ShapeDtypeStruct((rows, gq, width), bf16),
        in_specs=[pl.BlockSpec(memory_space=pltpu.SMEM), pl.BlockSpec(memory_space=pltpu.VMEM), hbm, hbm, hbm,
                  pl.BlockSpec((1,) + ckv.shape[1:], lambda i: (row(i), 0, 0)),
                  pl.BlockSpec((1,) + kr.shape[1:], lambda i: (row(i), 0, 0))],
        out_specs=pl.BlockSpec((1, gq, width), lambda i: (jnp.maximum(i - LAG_D, 0), 0, 0)),
        scratch_shapes=[
            pltpu.VMEM((2, dim, 2, nope), bf16), pltpu.VMEM((4, 2) + wr.shape[1:], bf16), pltpu.VMEM(w_uk.shape, bf16),
            pltpu.VMEM((CUTS, 2 * rows * toks, 2 * dim // CUTS), bf16), pltpu.VMEM((2 * rows * toks, 2 * nope), f32),
            pltpu.VMEM((rows, 2, chips, gq, width), bf16), pltpu.VMEM((rows, 2, chips, gq // 2, 128), bf16),
            pltpu.VMEM((2, nq, local_len), f32), pltpu.VMEM((2, nq, local_len), bf16),
            pltpu.VMEM((AWAY, chips, gq, width), f32), pltpu.VMEM((rows + 1, chips, 1, 128), f32),
            pltpu.VMEM((HOME + 1, chips, gq, width), f32), pltpu.VMEM((rows + 1, chips, 1, 128), f32),
            pltpu.VMEM((PAIR + 1, chips, gq, width), f32), pltpu.VMEM((rows + 1, chips, 1, 128), f32),
            pltpu.VMEM((ONE + 1, 2, gq // 2, width), f32), pltpu.VMEM((rows + 1, 2, 1, 128), f32),
            pltpu.VMEM((TWO + 1, 2, gq, width), f32), pltpu.VMEM((rows + 1, 2, 1, 128), f32),
            dma((heads // 4, 2, CUTS)), dma((2, heads // 2)), dma(()), dma((8, 7)), dma((8, 7)),
            dma((rows, 10)), dma((rows, 10))],
        compiler_params=pltpu.CompilerParams(collective_id=1, has_side_effects=True,
                                             dimension_semantics=("arbitrary",), vmem_limit_bytes=67_000_000),
        name="attend_merge",
    )(lens, hidden, wq, wr, w_uk, ckv, kr)


def unpack(ref, slot):
    rows = ref.shape[0]
    tiles = [ref[b, pl.ds(slot, 16)].astype(jnp.float32) for b in range(rows)]
    vals = []
    for h in range(2):
        even = jnp.concatenate([t[8 * h:8 * h + 8] for t in tiles[0::2]], axis=0)
        odd = jnp.concatenate([t[8 * h:8 * h + 8] for t in tiles[1::2]], axis=0)
        n = even.shape[0]
        low = lax.rem(lax.broadcasted_iota(jnp.int32, even.shape, 0), 8) < 4
        vals += [jnp.where(low, even, pltpu.roll(odd, 4, 0)), jnp.where(low, pltpu.roll(even, n - 4, 0), odd)]
    return [v.astype(ref.dtype) for v in vals]


def output_kernel(chips, o_ref, hid_ref, wv_ref, w_ref, out_ref, o_buf, hid_buf, wv_buf, ov, w_buf,
                  away, near, home, one, two, in_sem, w_sem, send, recv):
    x, c, xr, xl, right, left, partner = place(chips)
    xo = lax.rem(x + 2, chips)
    cols = w_buf.shape[2]
    rows, toks = out_ref.shape[:2]
    span = lambda dev: pl.ds(pl.multiple_of(dev * cols, 128), cols)
    dests = (xo, xr, xl, x)
    order = []
    for k in range(chips):
        order += [2 * dests[k] + 1 - c, 2 * dests[k] + c]

    def load(n):
        return pltpu.make_async_copy(w_ref.at[:, span(order[n])], w_buf.at[n], w_sem.at[n])

    firsts = [pltpu.make_async_copy(o_ref, o_buf, in_sem.at[0]), pltpu.make_async_copy(wv_ref, wv_buf, in_sem.at[1]),
              pltpu.make_async_copy(hid_ref.at[:, :, span(2 * x + c)], hid_buf, in_sem.at[2])]
    for cp in firsts:
        cp.start()
    for n in range(AHEAD):
        load(n).start()
    greet((right, left, partner))

    firsts[0].wait()
    firsts[1].wait()
    value = wv_buf.shape[2]
    for q in range(wv_buf.shape[0] // 4):
        for h, o_lat in enumerate(unpack(o_buf, 16 * q)):
            ov[:, pl.ds((4 * q + h) * value, value)] = jnp.dot(
                o_lat, wv_buf[4 * q + h], preferred_element_type=jnp.float32).astype(ov.dtype)

    tokens = ov.shape[0]
    first, second = pl.ds(0, tokens // 2), pl.ds(tokens // 2, tokens // 2)

    def project(n):
        load(n).wait()
        if n + AHEAD < 2 * chips:
            load(n + AHEAD).start()
        return jnp.dot(ov[...], w_buf[n], preferred_element_type=jnp.float32)

    def swap(k):
        return remote(away.at[k], near.at[k], send.at[0, k], recv.at[0, k], partner)

    def hop(kind):
        src, dst, dev = ((home.at[0, first], one.at[0], right), (home.at[0, second], one.at[1], left),
                         (home.at[1], two.at[0], right), (home.at[2], two.at[1], left))[kind]
        return remote(src, dst, send.at[1, kind], recv.at[1, kind], dev)

    away[0] = project(0)
    swap(0).start()
    for k in range(chips):
        home[k] = project(2 * k + 1)
        if k + 1 < chips:
            away[k + 1] = project(2 * k + 2)
            swap(k + 1).start()
        swap(k).wait_recv()
        home[k] = home[k] + near[k]
        if k == 0:
            hop(0).start()
            hop(1).start()
        if k == 1:
            hop(0).wait_recv()
            home[1, first] = home[1, first] + one[0]
            hop(2).start()
        if k == 2:
            hop(1).wait_recv()
            home[2, second] = home[2, second] + one[1]
            hop(3).start()
    firsts[2].wait()
    hop(2).wait_recv()
    hop(3).wait_recv()
    y = home[chips - 1] + two[0] + two[1]
    out_ref[:, :, span(2 * x + c)] = (hid_buf[...].astype(jnp.float32) + y.reshape(rows, toks, cols)).astype(out_ref.dtype)

    whole, top, low = pl.ds(0, rows), pl.ds(0, rows // 2), pl.ds(rows // 2, rows // 2)

    def give(kind, part, block, core, dev):
        ref = out_ref.at[part, :, span(2 * block + core)]
        return remote(ref, ref, send.at[2, kind], recv.at[2, kind], dev)

    sends = [give(0, whole, x, c, right), give(1, whole, x, c, left), give(2, whole, x, c, partner),
             give(3, top, xl, c, right), give(4, low, xr, c, left),
             give(5, whole, xl, c, partner), give(6, whole, xr, c, partner),
             give(7, top, xo, c, partner), give(8, low, xo, c, partner)]
    for n in (0, 1, 2):
        sends[n].start()
    give(0, whole, xl, c, partner).wait_recv()
    sends[3].start()
    sends[5].start()
    give(1, whole, xr, c, partner).wait_recv()
    sends[4].start()
    sends[6].start()
    give(3, top, xo, c, partner).wait_recv()
    sends[7].start()
    give(4, low, xo, c, partner).wait_recv()
    sends[8].start()
    for kind, part, block in ((2, whole, x), (5, whole, xl), (6, whole, xr), (7, top, xo), (8, low, xo)):
        give(kind, part, block, 1 - c, partner).wait_recv()
    for k in range(chips):
        swap(k).wait_send()
        hop(k).wait_send()
    for cp in sends:
        cp.wait_send()


def output(chips, o_lat, hidden, w_uv, w_o):
    rows, toks, dim = hidden.shape
    tokens = rows * toks
    depth = w_o.shape[0]
    cols = dim // (2 * chips)
    f32 = jnp.float32
    vmem, hbm = pl.BlockSpec(memory_space=pltpu.VMEM), pl.BlockSpec(memory_space=pl.ANY)
    dma = pltpu.SemaphoreType.DMA
    return pl.pallas_call(
        functools.partial(output_kernel, chips),
        out_shape=jax.ShapeDtypeStruct(hidden.shape, hidden.dtype),
        in_specs=[hbm] * 4,
        out_specs=vmem,
        scratch_shapes=[
            pltpu.VMEM(o_lat.shape, o_lat.dtype), pltpu.VMEM((rows, toks, cols), hidden.dtype),
            pltpu.VMEM(w_uv.shape, w_uv.dtype), pltpu.VMEM((tokens, depth), o_lat.dtype),
            pltpu.VMEM((2 * chips, depth, cols), w_o.dtype),
            pltpu.VMEM((chips, tokens, cols), f32), pltpu.VMEM((chips, tokens, cols), f32),
            pltpu.VMEM((chips, tokens, cols), f32), pltpu.VMEM((2, tokens // 2, cols), f32),
            pltpu.VMEM((2, tokens, cols), f32),
            dma((3,)), dma((2 * chips,)), dma((3, 9)), dma((3, 9))],
        compiler_params=pltpu.CompilerParams(collective_id=2, has_side_effects=True, vmem_limit_bytes=60_000_000),
        name="project_output",
    )(o_lat, hidden, w_uv, w_o)


def solution(mesh):
    chips = mesh.shape["seq"] // 2

    def local_step(hidden, cache_lens, c_kv, k_r, w_uq, w_qr, w_uk, w_uv, w_o):
        rows, toks, dim = hidden.shape
        heads, nope, width = w_uk.shape
        rope_dim = w_qr.shape[2]
        value = w_uv.shape[2]
        score_scale = (nope + rope_dim) ** -0.5
        o_lat = attend(chips, score_scale, cache_lens, hidden, w_uq, w_qr, w_uk, c_kv, jnp.swapaxes(k_r, 1, 2))
        return output(chips, o_lat, hidden, w_uv, w_o.reshape(heads * value, dim))

    specs_in = (P("batch", None, None), P("batch"), P("batch", "seq", None), P("batch", "seq", None),
                P(None, "seq", None), P(None, "seq", None), P("seq", None, None), P("seq", None, None),
                P("seq", None, None))
    return jax.shard_map(local_step, mesh=mesh, in_specs=specs_in, out_specs=P("batch", None, None), check_vma=False)
```

time: 174 us -> 169 us (0.971)
  Pallas kernels: 172 us -> 166 us
    pallas_call x1 -> x0, Pallas kernels: 52.4 us -> none  [queries(): pl.pallas_call(functools.partial(query_kernel, chips), out_shape=[jax.Sha...]
    pallas_call x1, Pallas kernels: 91 us -> 137 us  [attend(): pl.pallas_call(functools.partial(attend_kernel, chips, rows, scale), grid...]
where the time goes in v4:
time: 169 us; the launch traced here: 168 us
  Pallas kernels  166 us (98%)
  local copies, waits for them, and re-layouts  2.42 us (1%)
    pallas_call x1, Pallas kernels, attend(): pl.pallas_call(functools.partial(attend_kernel, chips, rows, scale), grid...  137 us
    pallas_call x1, Pallas kernels, output(): pl.pallas_call(functools.partial(output_kernel, chips), out_shape=jax.Sha...  28.1 us

profile of v4, /device:TPU:113, one launch (start us, length us, event | category | flops | bytes accessed | tf_op | source)
XLA Modules:
  0.0 168.0 jit_solution(7285397105798425483)
XLA Ops:
  0.0 137.4 %attend_merge.1.o_ref = bf16[16,64,512]{2,1,0:T(8,128)(2,1)} custom-call(s32[16]{0:T(128)} %lens_ref.1, bf16[16,4,7168]{2,1,0:T(4,128)(2,1)} %hid_ref.3, bf16[7168,8,2,128]{3,2,1,0:T(2,128)(2,1)} %bitcast.4, bf16[16,64,7168]{2,1,0:T(8,128)(2,1)} %bitcast.6, bf16[16,128,512]{2,1,0:T(8,128)(2,1)} %wk_ref.1, bf16[16,2048,512]{2,1,0:T(8,128)(2,1)} %ckv_ref.1, ...), custom_call_target="tpu_custom_call" | custom-call | tf_op jit(solution)/shard_map/attend_merge/pallas_call | solution.py:405
  137.4 28.1 %project_output.1 = bf16[16,4,7168]{2,1,0:T(4,128)(2,1)} custom-call(bf16[16,64,512]{2,1,0:T(8,128)(2,1)} %attend_merge.1.o_ref, bf16[16,4,7168]{2,1,0:T(4,128)(2,1)} %hid_ref.3, bf16[16,512,128]{2,1,0:T(8,128)(2,1)} %wv_ref.1, bf16[2048,7168]{1,0:T(8,128)(2,1)} %bitcast.5), custom_call_target="tpu_custom_call" | custom-call | tf_op jit(solution)/shard_map/project_output/pallas_call | solution.py:557
  165.6 2.4 %copy.11 = bf16[16,4,7168]{2,1,0:T(4,128)(2,1)} copy(bf16[16,4,7168]{2,1,0:T(4,128)(2,1)} %project_output.1) | data formatting | bytes 1835008

commit v5 on v4

--- a/solution.py
+++ b/solution.py
@@ -13,7 +13,7 @@
 LAG_B, LAG_C, LAG_D = 1, 3, 6
 CUTS = 4
 AHEAD = 3
-AWAY, HOME, PAIR, ONE, TWO = 4, 10, 4, 6, 8
+AWAY, HOME, PAIR, ONE, TWO = 4, 10, 4, 4, 6
 
 
 def remote(src, dst, send_sem, recv_sem, dev):
@@ -62,7 +62,7 @@
 def attend_kernel(chips, rows, scale, lens_ref, hid_ref, wq_ref, wr_ref, wk_ref, ckv_ref, kr_ref, out_ref,
                   wq_buf, wr_buf, wk_buf, wide, acc, lat_all, rope_all, s_buf, p_buf,
                   away_o, away_ml, home_o, home_ml, d2d_o, d2d_ml, one_o, one_ml, two_o, two_ml,
-                  wq_sem, wr_sem, wk_sem, q_send, q_recv, send, recv):
+                  wq_sem, wr_sem, wk_sem, q_send, q_recv, send0, send1, send2, recv0, recv1, recv2):
     x, c, xr, xl, right, left, partner = place(chips)
     xo = lax.rem(x + 2, chips)
     i = pl.program_id(0)
@@ -79,7 +79,8 @@
     k2 = scale * LOG2E
     lanes = [pl.ds(j * 128, 128) for j in range(width // 128)]
 
-    top, low, every = pl.ds(0, rows // 2), pl.ds(rows // 2, rows // 2), pl.ds(0, rows)
+    early = rows // 4
+    top, low, every = pl.ds(0, early), pl.ds(early, rows - early), pl.ds(0, rows)
     pieces = [(lat_all, every, pl.ds(0, 16), 0), (lat_all, every, pl.ds(16, 16), 1)]
     for part, turn in ((top, 0), (low, 1)):
         pieces += [(lat_all, part, pl.ds(32, 16), 0), (lat_all, part, pl.ds(48, 16), 1),
@@ -132,10 +133,10 @@
 
         def load(q, h, k):
             at = pl.ds(k * depth, depth)
-            return pltpu.make_async_copy(wq_ref.at[at, 2 * q + h], wq_buf.at[h, at], wq_sem.at[q, h, k])
+            return pltpu.make_async_copy(wq_ref.at[at, 2 * q + h], wq_buf.at[h, at], wq_sem.at[h, k])
 
         def load_rope(half, j):
-            return pltpu.make_async_copy(wr_ref.at[half * pairs + j], wr_buf.at[j % 4, half], wr_sem.at[half, j])
+            return pltpu.make_async_copy(wr_ref.at[half * pairs + j], wr_buf.at[j % 4, half], wr_sem.at[half, j % 4])
 
         load_up = pltpu.make_async_copy(wk_ref, wk_buf, wk_sem)
         for k in range(CUTS):
@@ -162,26 +163,32 @@
         for q in range(quarters):
             acc[...] = jnp.zeros_like(acc)
 
-            @pl.loop(0, CUTS)
+            @pl.loop(0, CUTS // 2)
             def _(k):
                 for h in range(2):
-                    load(q, h, k).wait()
-                w = [wq_buf[h, pl.ds(k * depth, depth)].reshape(2 * depth, nope) for h in range(2)]
-                acc[...] += jnp.dot(wide[k], jnp.concatenate(w, axis=1), preferred_element_type=f32)
+                    for e in range(2):
+                        load(q, h, 2 * k + e).wait()
+                for e in range(2):
+                    w = [wq_buf.at[h, pl.ds((2 * k + e) * depth, depth)].reshape(2 * depth, nope)[...] for h in range(2)]
+                    acc[e] += jnp.dot(wide[2 * k + e], jnp.concatenate(w, axis=1), preferred_element_type=f32)
                 if q < quarters - 1:
-                    for h in range(2):
-                        load(q + 1, h, k).start()
+                    for e in range(2):
+                        for h in range(2):
+                            load(q + 1, h, 2 * k + e).start()
 
             if q == 0:
                 load_up.wait()
             q_lat = []
             for h in range(4):
-                q_n = acc[pl.ds((h % 2) * n, n), pl.ds((h // 2) * nope, nope)].astype(bf16)
+                at = (pl.ds((h % 2) * n, n), pl.ds((h // 2) * nope, nope))
+                q_n = (acc[0, *at] + acc[1, *at]).astype(bf16)
                 q_lat.append(jnp.dot(q_n, wk_buf[4 * q + h], preferred_element_type=f32))
             pack(q_lat, lat_all.at[:, c, x], q * 16)
             if q == 0:
                 pl.semaphore_wait(barrier, 3)
             send_own(q)
+            if q == quarters - 1:
+                relay(0)
 
         tokens = jnp.concatenate([hid_ref[:, :, t * 128:(t + 1) * 128].reshape(n, 128) for t in range(dim // 128)],
                                  axis=1)
@@ -199,8 +206,10 @@
                         load_rope(half, 2 * m + 5).start()
                 q_rope += [r[:, 0:128], r[:, 128:256]]
             pack(q_rope, rope_all.at[:, c, x], 16 * q)
+            if q == 0:
+                relay(1)
         send_own(4)
-        for p in range(5):
+        for p in range(2, 5):
             relay(p)
         for p in range(5, 8):
             send_own(p)
@@ -226,7 +235,10 @@
 
     def copy(r, kind):
         src, dst, dev = moves(r)[kind]
-        return remote(src, dst, send.at[r, kind], recv.at[r, kind], dev)
+        out, into, count, first = ((send0, recv0, PAIR, 0) if kind < 2 else (send1, recv1, ONE, 2) if kind < 6
+                                   else (send2, recv2, TWO, 6))
+        at = (lax.rem(r, count), kind - first)
+        return remote(src, dst, out.at[at], into.at[at], dev)
 
     def late(lag):
         return jnp.where((i >= lag) & (i < rows + lag), i - lag, rows)
@@ -288,20 +300,14 @@
     def _():
         make_queries()
 
-    @pl.when(i == rows // 2)
+    @pl.when(i == early)
     def _():
         for p in range(5, 8):
             complete(p)
 
-    @pl.when((i >= AWAY) & (i < rows + AWAY))
-    def _():
-        for kind in range(0, 2):
-            copy(i - AWAY, kind).wait_send()
-
-    @pl.when(i >= HOME)
-    def _():
-        for kind in range(2, 10):
-            copy(i - HOME, kind).wait_send()
+    on_row(AWAY, lambda cp: cp.wait_send(), range(0, 2))
+    on_row(LAG_B + ONE, lambda cp: cp.wait_send(), range(2, 6))
+    on_row(LAG_C + TWO, lambda cp: cp.wait_send(), range(6, 10))
 
     on_row(LAG_D, lambda cp: cp.wait_recv(), range(6, 10))
 
@@ -384,10 +390,10 @@
         for p in range(8):
             sent(p)
 
-        @pl.loop(rows + LAG_D - HOME, rows)
-        def _(r):
-            for kind in range(2, 10):
-                copy(r, kind).wait_send()
+        for lag, kinds in ((LAG_B + ONE, range(2, 6)), (LAG_C + TWO, range(6, 10))):
+            for r in range(rows + LAG_D - lag, rows):
+                for kind in kinds:
+                    copy(r, kind).wait_send()
 
 
 def attend(chips, scale, lens, hidden, w_uq, w_qr, w_uk, ckv, kr):
@@ -412,7 +418,7 @@
         out_specs=pl.BlockSpec((1, gq, width), lambda i: (jnp.maximum(i - LAG_D, 0), 0, 0)),
         scratch_shapes=[
             pltpu.VMEM((2, dim, 2, nope), bf16), pltpu.VMEM((4, 2) + wr.shape[1:], bf16), pltpu.VMEM(w_uk.shape, bf16),
-            pltpu.VMEM((CUTS, 2 * rows * toks, 2 * dim // CUTS), bf16), pltpu.VMEM((2 * rows * toks, 2 * nope), f32),
+            pltpu.VMEM((CUTS, 2 * rows * toks, 2 * dim // CUTS), bf16), pltpu.VMEM((2, 2 * rows * toks, 2 * nope), f32),
             pltpu.VMEM((rows, 2, chips, gq, width), bf16), pltpu.VMEM((rows, 2, chips, gq // 2, 128), bf16),
             pltpu.VMEM((2, nq, local_len), f32), pltpu.VMEM((2, nq, local_len), bf16),
             pltpu.VMEM((AWAY, chips, gq, width), f32), pltpu.VMEM((rows + 1, chips, 1, 128), f32),
@@ -420,8 +426,8 @@
             pltpu.VMEM((PAIR + 1, chips, gq, width), f32), pltpu.VMEM((rows + 1, chips, 1, 128), f32),
             pltpu.VMEM((ONE + 1, 2, gq // 2, width), f32), pltpu.VMEM((rows + 1, 2, 1, 128), f32),
             pltpu.VMEM((TWO + 1, 2, gq, width), f32), pltpu.VMEM((rows + 1, 2, 1, 128), f32),
-            dma((heads // 4, 2, CUTS)), dma((2, heads // 2)), dma(()), dma((8, 7)), dma((8, 7)),
-            dma((rows, 10)), dma((rows, 10))],
+            dma((2, CUTS)), dma((2, 4)), dma(()), dma((8, 7)), dma((8, 7))]
+            + 2 * [dma((PAIR, 2)), dma((ONE, 4)), dma((TWO, 4))],
         compiler_params=pltpu.CompilerParams(collective_id=1, has_side_effects=True,
                                              dimension_semantics=("arbitrary",), vmem_limit_bytes=67_000_000),
         name="attend_merge",
@@ -486,32 +492,33 @@
 
     def hop(kind):
         src, dst, dev = ((home.at[0, first], one.at[0], right), (home.at[0, second], one.at[1], left),
-                         (home.at[1], two.at[0], right), (home.at[2], two.at[1], left))[kind]
+                         (home.at[1, second], two.at[0, second], right), (home.at[2, first], two.at[1, first], left),
+                         (home.at[1, first], two.at[0, first], right),
+                         (home.at[2, second], two.at[1, second], left))[kind]
         return remote(src, dst, send.at[1, kind], recv.at[1, kind], dev)
 
     away[0] = project(0)
     swap(0).start()
     for k in range(chips):
         home[k] = project(2 * k + 1)
+        swap(k).wait_recv()
+        home[k] = home[k] + near[k]
+        for kind in ((0, 1), (2,), (3,), ())[k]:
+            hop(kind).start()
         if k + 1 < chips:
             away[k + 1] = project(2 * k + 2)
             swap(k + 1).start()
-        swap(k).wait_recv()
-        home[k] = home[k] + near[k]
-        if k == 0:
-            hop(0).start()
-            hop(1).start()
         if k == 1:
             hop(0).wait_recv()
             home[1, first] = home[1, first] + one[0]
-            hop(2).start()
+            hop(4).start()
         if k == 2:
             hop(1).wait_recv()
             home[2, second] = home[2, second] + one[1]
-            hop(3).start()
+            hop(5).start()
     firsts[2].wait()
-    hop(2).wait_recv()
-    hop(3).wait_recv()
+    for kind in range(2, 6):
+        hop(kind).wait_recv()
     y = home[chips - 1] + two[0] + two[1]
     out_ref[:, :, span(2 * x + c)] = (hid_buf[...].astype(jnp.float32) + y.reshape(rows, toks, cols)).astype(out_ref.dtype)
 
@@ -521,27 +528,22 @@
         ref = out_ref.at[part, :, span(2 * block + core)]
         return remote(ref, ref, send.at[2, kind], recv.at[2, kind], dev)
 
-    sends = [give(0, whole, x, c, right), give(1, whole, x, c, left), give(2, whole, x, c, partner),
-             give(3, top, xl, c, right), give(4, low, xr, c, left),
-             give(5, whole, xl, c, partner), give(6, whole, xr, c, partner),
-             give(7, top, xo, c, partner), give(8, low, xo, c, partner)]
-    for n in (0, 1, 2):
-        sends[n].start()
-    give(0, whole, xl, c, partner).wait_recv()
-    sends[3].start()
-    sends[5].start()
-    give(1, whole, xr, c, partner).wait_recv()
-    sends[4].start()
-    sends[6].start()
-    give(3, top, xo, c, partner).wait_recv()
-    sends[7].start()
-    give(4, low, xo, c, partner).wait_recv()
-    sends[8].start()
-    for kind, part, block in ((2, whole, x), (5, whole, xl), (6, whole, xr), (7, top, xo), (8, low, xo)):
+    sends = [give(0, top, x, c, right), give(1, low, x, c, right), give(2, low, x, c, left), give(3, top, x, c, left),
+             give(4, whole, x, c, partner), give(5, top, xl, c, right), give(6, low, xr, c, left),
+             give(7, whole, xl, c, partner), give(8, whole, xr, c, partner),
+             give(9, top, xo, c, partner), give(10, low, xo, c, partner)]
+    for k in (0, 2, 1, 3, 4):
+        sends[k].start()
+    for kind, part, block, then in ((0, top, xl, 5), (2, low, xr, 6), (1, low, xl, 7), (3, top, xr, 8),
+                                    (5, top, xo, 9), (6, low, xo, 10)):
+        give(kind, part, block, c, partner).wait_recv()
+        sends[then].start()
+    for kind, part, block in ((4, whole, x), (7, whole, xl), (8, whole, xr), (9, top, xo), (10, low, xo)):
         give(kind, part, block, 1 - c, partner).wait_recv()
     for k in range(chips):
         swap(k).wait_send()
-        hop(k).wait_send()
+    for kind in range(6):
+        hop(kind).wait_send()
     for cp in sends:
         cp.wait_send()
 
@@ -566,8 +568,8 @@
             pltpu.VMEM((chips, tokens, cols), f32), pltpu.VMEM((chips, tokens, cols), f32),
             pltpu.VMEM((chips, tokens, cols), f32), pltpu.VMEM((2, tokens // 2, cols), f32),
             pltpu.VMEM((2, tokens, cols), f32),
-            dma((3,)), dma((2 * chips,)), dma((3, 9)), dma((3, 9))],
-        compiler_params=pltpu.CompilerParams(collective_id=2, has_side_effects=True, vmem_limit_bytes=60_000_000),
+            dma((3,)), dma((2 * chips,)), dma((3, 11)), dma((3, 11))],
+        compiler_params=pltpu.CompilerParams(collective_id=2, has_side_effects=True, vmem_limit_bytes=65_500_000),
         name="project_output",
     )(o_lat, hidden, w_uv, w_o)
 

time: 169 us -> 161 us (0.953)
  Pallas kernels: 166 us -> 159 us
    pallas_call x1, Pallas kernels: 137 us -> 132 us  [attend(): pl.pallas_call(functools.partial(attend_kernel, chips, rows, scale), grid...]
where the time goes in v5:
time: 161 us
  Pallas kernels  159 us (99%)
  local copies, waits for them, and re-layouts  2.42 us (2%)
    pallas_call x1, Pallas kernels, attend(): pl.pallas_call(functools.partial(attend_kernel, chips, rows, scale), grid...  132 us
    pallas_call x1, Pallas kernels, output(): pl.pallas_call(functools.partial(output_kernel, chips), out_shape=jax.Sha...  26.8 us

profile of v5, /device:TPU:113, one launch (start us, length us, event | category | flops | bytes accessed | tf_op | source)
XLA Modules:
  0.0 161.1 jit_solution(706350140474541347)
XLA Ops:
  0.0 131.9 %attend_merge.1.o_ref = bf16[16,64,512]{2,1,0:T(8,128)(2,1)} custom-call(s32[16]{0:T(128)} %lens_ref.1, bf16[16,4,7168]{2,1,0:T(4,128)(2,1)} %hid_ref.3, bf16[7168,8,2,128]{3,2,1,0:T(2,128)(2,1)} %bitcast.4, bf16[16,64,7168]{2,1,0:T(8,128)(2,1)} %bitcast.6, bf16[16,128,512]{2,1,0:T(8,128)(2,1)} %wk_ref.1, bf16[16,2048,512]{2,1,0:T(8,128)(2,1)} %ckv_ref.1, ...), custom_call_target="tpu_custom_call" | custom-call | tf_op jit(solution)/shard_map/attend_merge/pallas_call | solution.py:411
  131.9 26.8 %project_output.1 = bf16[16,4,7168]{2,1,0:T(4,128)(2,1)} custom-call(bf16[16,64,512]{2,1,0:T(8,128)(2,1)} %attend_merge.1.o_ref, bf16[16,4,7168]{2,1,0:T(4,128)(2,1)} %hid_ref.3, bf16[16,512,128]{2,1,0:T(8,128)(2,1)} %wv_ref.1, bf16[2048,7168]{1,0:T(8,128)(2,1)} %bitcast.5), custom_call_target="tpu_custom_call" | custom-call | tf_op jit(solution)/shard_map/project_output/pallas_call | solution.py:559
  158.7 2.4 %copy.11 = bf16[16,4,7168]{2,1,0:T(4,128)(2,1)} copy(bf16[16,4,7168]{2,1,0:T(4,128)(2,1)} %project_output.1) | data formatting | bytes 1835008

commit v6 on v5

--- a/solution.py
+++ b/solution.py
@@ -143,9 +143,6 @@
             for h in range(2):
                 load(0, h, k).start()
         load_up.start()
-        for j in range(4):
-            for half in range(2):
-                load_rope(half, j).start()
 
         lane = lax.broadcasted_iota(jnp.int32, (128, 512), 1)
         src = lax.broadcasted_iota(jnp.int32, (128, 512), 0)
@@ -187,6 +184,10 @@
             if q == 0:
                 pl.semaphore_wait(barrier, 3)
             send_own(q)
+            if q == quarters - 3:
+                for j in range(4):
+                    for half in range(2):
+                        load_rope(half, j).start()
             if q == quarters - 1:
                 relay(0)
 
@@ -569,7 +570,7 @@
             pltpu.VMEM((chips, tokens, cols), f32), pltpu.VMEM((2, tokens // 2, cols), f32),
             pltpu.VMEM((2, tokens, cols), f32),
             dma((3,)), dma((2 * chips,)), dma((3, 11)), dma((3, 11))],
-        compiler_params=pltpu.CompilerParams(collective_id=2, has_side_effects=True, vmem_limit_bytes=65_500_000),
+        compiler_params=pltpu.CompilerParams(collective_id=2, has_side_effects=True, vmem_limit_bytes=55_000_000),
         name="project_output",
     )(o_lat, hidden, w_uv, w_o)
 

time: 161 us -> 159 us (0.988)
  no operation moved by 1% of the time
where the time goes in v6:
time: 159 us; the launch traced here: 158 us
  Pallas kernels  158 us (99%)
    pallas_call x1, Pallas kernels, attend(): pl.pallas_call(functools.partial(attend_kernel, chips, rows, scale), grid...  132 us
    pallas_call x1, Pallas kernels, output(): pl.pallas_call(functools.partial(output_kernel, chips), out_shape=jax.Sha...  25.8 us

profile of v6, /device:TPU:113, one launch (start us, length us, event | category | flops | bytes accessed | tf_op | source)
XLA Modules:
  0.0 158.5 jit_solution(6805897731096032200)
XLA Ops:
  0.0 131.7 %attend_merge.1.o_ref = bf16[16,64,512]{2,1,0:T(8,128)(2,1)} custom-call(s32[16]{0:T(128)} %lens_ref.1, bf16[16,4,7168]{2,1,0:T(4,128)(2,1)} %hid_ref.3, bf16[7168,8,2,128]{3,2,1,0:T(2,128)(2,1)} %bitcast.4, bf16[16,64,7168]{2,1,0:T(8,128)(2,1)} %bitcast.6, bf16[16,128,512]{2,1,0:T(8,128)(2,1)} %wk_ref.1, bf16[16,2048,512]{2,1,0:T(8,128)(2,1)} %ckv_ref.1, ...), custom_call_target="tpu_custom_call" | custom-call | tf_op jit(solution)/shard_map/attend_merge/pallas_call | solution.py:412
  131.7 25.8 %project_output.1 = bf16[16,4,7168]{2,1,0:T(4,128)(2,1)S(1)} custom-call(bf16[16,64,512]{2,1,0:T(8,128)(2,1)} %attend_merge.1.o_ref, bf16[16,4,7168]{2,1,0:T(4,128)(2,1)} %hid_ref.3, bf16[16,512,128]{2,1,0:T(8,128)(2,1)} %wv_ref.1, bf16[2048,7168]{1,0:T(8,128)(2,1)} %bitcast.5), custom_call_target="tpu_custom_call" | custom-call | tf_op jit(solution)/shard_map/project_output/pallas_call | solution.py:560
  157.6 0.9 copy.11
